TPU v7x, 32 devices: a whole 2x2x4 slice. The times are simulated.
32 devices in a mesh: bank: 4 (over x, core), zero: 8 (over z, y).
Axes of the slice: x: 2, y: 2, z: 4, core: 2. Of those that a mesh axis runs over, the one named last changes fastest.
Arguments:
- w_gate: float32 [64, 2048, 1024], P('bank', 'zero'), may hold values from -0.1875 to 0.1875
- avg_gate: float32 [64, 2048, 1024], P('bank', 'zero'), may hold values from -0.125 to 0.125
- w_up: float32 [64, 2048, 1024], P('bank', 'zero'), may hold values from -0.1875 to 0.1875
- avg_up: float32 [64, 2048, 1024], P('bank', 'zero'), may hold values from -0.125 to 0.125
- mix_share: float32 [64], P('bank'), may hold values from 0.2 to 0.8
- router_weight: float32 [2048, 64], P('zero', 'bank'), may hold values from -0.125 to 0.125
- router_gain: float32 [2048], P('zero'), may hold values from 0.25 to 1.75
Outputs:
- serve_gate: bfloat16 [64, 2048, 1024], P('bank', None, 'zero')
- serve_up: bfloat16 [64, 2048, 1024], P('bank', None, 'zero')
- scale_gate: float32 [64, 1024], P('bank', 'zero')
- scale_up: float32 [64, 1024], P('bank', 'zero')
- serve_router: bfloat16 [2048, 64], replicated
All inputs are finite; a program needn't handle non-finite values. Where the computation divides by a largest or mean magnitude, that divisor is 1e-20 or more.
Results may differ from a plain program's by a relative error of at most 0.001.
Values may be sent and summed in bfloat16 or wider, within the bound.
No kernel may reach another device: no remote copies, remote signals or barrier semaphores. Data moves between devices by JAX's collectives and lax.ppermute only.
A program may use at most 256 MiB of HBM per device.

v0:
```python
import jax
import jax.numpy as jnp
from jax import lax
from jax.sharding import PartitionSpec as P

D_MODEL = 2048


def on_device(w_gate, avg_gate, w_up, avg_up, mix_share, router_weight, router_gain):
    fresh_gate = mix_share[:, None, None] * w_gate + (1.0 - mix_share[:, None, None]) * avg_gate
    fresh_up = mix_share[:, None, None] * w_up + (1.0 - mix_share[:, None, None]) * avg_up
    total_gate, total_up = lax.psum(
        (jnp.sum(jnp.abs(fresh_gate), axis=1), jnp.sum(jnp.abs(fresh_up), axis=1)), "zero"
    )
    scale_gate = total_gate / D_MODEL
    scale_up = total_up / D_MODEL
    narrow_gate, narrow_up = (
        (fresh_gate / jnp.expand_dims(scale_gate, 1)).astype(jnp.bfloat16),
        (fresh_up / jnp.expand_dims(scale_up, 1)).astype(jnp.bfloat16),
    )
    serve_gate, serve_up = (
        lax.all_to_all(narrow_gate, "zero", split_axis=2, concat_axis=1, tiled=True),
        lax.all_to_all(narrow_up, "zero", split_axis=2, concat_axis=1, tiled=True),
    )
    scale_gate = lax.dynamic_slice_in_dim(
        scale_gate, lax.axis_index("zero") * serve_gate.shape[2], serve_gate.shape[2], axis=1
    )
    scale_up = lax.dynamic_slice_in_dim(
        scale_up, lax.axis_index("zero") * serve_up.shape[2], serve_up.shape[2], axis=1
    )
    part_router = (router_weight * router_gain[:, None]).astype(jnp.bfloat16)
    row_router = lax.all_gather(part_router, "zero", axis=0, tiled=True)
    serve_router = lax.all_gather(row_router, "bank", axis=1, tiled=True)
    return (serve_gate, serve_up, scale_gate, scale_up, serve_router)


def solution(mesh):
    in_specs = (
        P("bank", "zero", None),
        P("bank", "zero", None),
        P("bank", "zero", None),
        P("bank", "zero", None),
        P("bank"),
        P("zero", "bank"),
        P("zero"),
    )
    out_specs = (
        P("bank", None, "zero"),
        P("bank", None, "zero"),
        P("bank", "zero"),
        P("bank", "zero"),
        P(),
    )
    return jax.shard_map(
        on_device, mesh=mesh, in_specs=in_specs, out_specs=out_specs, check_vma=False
    )
```

profile of v0, /device:TPU:0, one launch (start us, length us, event | category | flops | bytes accessed | tf_op | source)
XLA Modules:
  0.0 642.4 jit_solution(310486662684483789)
XLA Ops:
  7.2 0.0 all-reduce.3.cloned.1.call-start
  7.2 17.6 %copy.22 = f32[16,256,1024]{1,0,2:T(8,128)} copy(f32[16,256,1024]{2,1,0:T(8,128)} %param.7) | data formatting | bytes 33554432 | tf_op args[0]
  24.8 17.6 %copy.23 = f32[16,256,1024]{1,0,2:T(8,128)} copy(f32[16,256,1024]{2,1,0:T(8,128)} %param.8) | data formatting | bytes 33554432 | tf_op args[1]
  42.4 17.6 %copy.25 = f32[16,256,1024]{1,0,2:T(8,128)} copy(f32[16,256,1024]{2,1,0:T(8,128)} %param.9) | data formatting | bytes 33554432 | tf_op args[2]
  60.0 0.0 copy-start.1
  60.0 17.6 %copy.26 = f32[16,256,1024]{1,0,2:T(8,128)} copy(f32[16,256,1024]{2,1,0:T(8,128)} %param.10) | data formatting | bytes 33554432 | tf_op args[3]
  77.6 0.0 copy-done.1
  77.6 23.7 %abs_reduce_fusion = (f32[16,1024]{0,1:T(8,128)}, f32[16,1024]{0,1:T(8,128)}) fusion(f32[16,256,1024]{1,0,2:T(8,128)} %copy.26, f32[16]{0:T(128)S(1)} %broadcast_subtract_fusion, f32[16,256,1024]{1,0,2:T(8,128)} %copy.25, f32[16]{0:T(128)S(1)} %copy-done.1, f32[16,256,1024]{1,0,2:T(8,128)} %copy.23, f32[16,256,1024]{1,0,2:T(8,128)} %copy.22), kind=kLoop, calls=%fused_computation.1 | loop fusion | flops 41910272 | bytes 67240064 | tf_op jit(solution)/shard_map/reduce_sum | solution.py:13
  101.3 0.0 all-reduce.3.cloned.1.call-update
  101.4 81.1 %all-reduce.3.cloned.1.call-done = (f32[16,1024]{0,1:T(8,128)}, f32[16,1024]{0,1:T(8,128)}) async-done(((f32[16,1024]{0,1:T(8,128)}, f32[16,1024]{0,1:T(8,128)}), (f32[16,1024]{0,1:T(8,128)}, f32[16,1024]{0,1:T(8,128)})) %all-reduce.3.cloned.1.call-update) | async-done | bytes 131088 | tf_op jit(solution)/shard_map/psum | solution.py:12
  182.5 1.3 broadcast_multiply_fusion
  183.8 25.3 %divide_convert_fusion = (bf16[16,256,1024]{1,0,2:T(8,128)(2,1)}, bf16[16,256,1024]{1,0,2:T(8,128)(2,1)S(1)}) fusion(f32[16,1024]{0,1:T(8,128)S(1)} %get-tuple-element.16, f32[16,256,1024]{1,0,2:T(8,128)} %copy.26, f32[16]{0:T(128)S(1)} %broadcast_subtract_fusion, f32[16,256,1024]{1,0,2:T(8,128)} %copy.25, f32[16]{0:T(128)S(1)} %copy-done.1, ...), kind=kLoop, calls=%fused_computation | loop fusion | flops 41943040 | bytes 84017280 | tf_op jit(solution)/shard_map/convert_element_type | solution.py:19
  209.1 0.0 copy-start
  209.1 0.0 copy-start.2
  209.1 187.1 %all_to_all.36 = bf16[16,256,1024]{1,0,2:T(8,128)(2,1)} all-to-all(bf16[16,256,1024]{1,0,2:T(8,128)(2,1)S(1)} %get-tuple-element.15), channel_id=1, replica_groups=mesh['bank'=4,'zero'=8] {'zero'}, dimensions={2} | all-to-all | bytes 16777216 | tf_op jit(solution)/shard_map/all_to_all | solution.py:22
  396.2 4.9 all-to-all-start.1
  401.1 0.0 copy-done
  401.1 0.0 copy-done.2
  401.1 202.0 %all_gather.6 = bf16[2048,16]{0,1:T(8,128)(2,1)S(1)} all-gather(bf16[256,16]{0,1:T(8,128)(2,1)S(1)} %multiply_convert_fusion), channel_id=1, replica_groups=mesh['bank'=4,'zero'=8] {'zero'}, dimensions={0}, use_global_device_ids=true | all-gather | bytes 73728 | tf_op jit(solution)/shard_map/all_gather | solution.py:32
  603.2 5.8 all_gather.7
  608.9 0.7 copy.28
  609.6 0.7 copy.29
  610.3 12.3 %copy.24 = bf16[16,8,256,128]{3,2,1,0:T(8,128)(2,1)} copy(bf16[16,8,256,128]{2,0,3,1:T(8,128)(2,1)} %bitcast.8) | data formatting | bytes 16777216 | tf_op jit(solution)/shard_map/all_to_all | solution.py:22
  622.6 0.0 all-to-all-done.1
  622.6 12.3 %copy.27 = bf16[16,8,256,128]{3,2,1,0:T(8,128)(2,1)} copy(bf16[16,8,256,128]{2,0,3,1:T(8,128)(2,1)} %bitcast.4) | data formatting | bytes 16777216 | tf_op jit(solution)/shard_map/all_to_all | solution.py:23
  634.8 0.7 copy.33
  (4 shorter events, 0.0 us)
Async XLA Ops:
  7.2 175.3 %all-reduce.3.cloned.1.call-start = ((), (), s32[]{:S(2)}) async-start(), calls=%async_computation.2 | async-start | bytes 2097152 | tf_op jit(solution)/shard_map/psum | solution.py:12
  60.0 17.6 %copy-start.1 = (f32[16]{0:T(128)S(1)}, f32[16]{0:T(128)}, u32[]{:S(2)}) copy-start(f32[16]{0:T(128)} %param.11) | copy-start | bytes 196
  209.1 192.0 %copy-start = (f32[256,16]{0,1:T(8,128)S(1)}, f32[256,16]{0,1:T(8,128)}, u32[]{:S(2)}) copy-start(f32[256,16]{0,1:T(8,128)} %param.12) | copy-start | bytes 49156
  209.1 192.0 %copy-start.2 = (f32[256]{0:T(256)S(1)}, f32[256]{0:T(256)}, u32[]{:S(2)}) copy-start(f32[256]{0:T(256)} %param.13) | copy-start | bytes 3076
  396.2 226.4 %all-to-all-start.1 = ((bf16[16,256,1024]{1,0,2:T(8,128)(2,1)}), bf16[16,256,1024]{1,0,2:T(8,128)(2,1)}, u32[]{:S(2)}, u32[]{:S(2)}) async-start(bf16[16,256,1024]{1,0,2:T(8,128)(2,1)} %get-tuple-element.14), calls=%async_computation.1 | async-start | bytes 16777216 | tf_op jit(solution)/shard_map/all_to_all | solution.py:23
Sparse Core Ops, SparseCore 0:
  101.5 80.9 all-reduce.2
where the time goes:
time: 644 us; the launch traced here: 642 us
  blocking collectives  395 us (61%)
  local copies, waits for them, and re-layouts  97 us (15%)
  waiting for transfers between devices  81.2 us (13%)
  other arithmetic  50.3 us (8%)
  between operations  14.1 us (2%)
    all_gather x1, blocking collectives, on_device(): row_router = lax.all_gather(part_router, 'zero', axis=0, tiled=True)  202 us
    all_to_all x1, blocking collectives, on_device(): lax.all_to_all(narrow_gate, 'zero', split_axis=2, concat_axis=1, tiled=True)  187 us
    psum x1, waiting for transfers between devices, on_device(): lax.psum((jnp.sum(jnp.abs(fresh_gate), axis=1), jnp.sum(jnp.abs(fresh_up)...  81.1 us
    unnamed x13, local copies, waits for them, and re-layouts  72.5 us
    convert_element_type x1, other arithmetic, on_device(): (fresh_up / jnp.expand_dims(scale_up, 1)).astype(jnp.bfloat16)  25.3 us
    reduce_sum x1, other arithmetic, on_device(): jnp.sum(jnp.abs(fresh_up), axis=1)  23.7 us
  transfers between devices with their start and end apart: 2, of which 1 were waited for; matrix products, arithmetic and copies ran while one was open for 2% of the time, Pallas kernels for 0%

commit v1 on v0

v1 whole, which is shorter than its diff:
```python
import functools

import jax
import jax.numpy as jnp
from jax import lax
from jax.experimental import pallas as pl
from jax.experimental.pallas import tpu as pltpu
from jax.sharding import PartitionSpec as P


GATE_GROUPS = ((4, 4), (4, 4))
UP_GROUPS = ((6, 6, 3, 1),)

SMEM = pl.BlockSpec(memory_space=pltpu.SMEM)
ANY = pl.BlockSpec(memory_space=pl.ANY)


def spans(groups, experts):
    whole = sum(map(sum, groups))
    at, out = 0, []
    for group in groups:
        chunks = []
        for share in group:
            first, last = at * experts // whole, (at + share) * experts // whole
            at += share
            if last > first:
                chunks.append((first, last - first))
        if chunks:
            out.append(chunks)
    return out


def step_of(most, *counts):
    return next(n for n in range(most, 0, -1) if all(count % n == 0 for count in counts))


def sums_body(first, step, mix_ref, w_ref, avg_ref, *refs):
    out_ref = refs[-1]
    for i in range(step):
        at = pl.program_id(0) * step + i
        mix = mix_ref[first + at]
        fresh = mix * w_ref[i] + (1.0 - mix) * avg_ref[i]
        out_ref[pl.ds(at, 1), :] = jnp.sum(jnp.abs(fresh), axis=0, keepdims=True)


def sums(mix, w, avg, first, count):
    _, rows, cols = w.shape
    step = step_of(4 if first else 2, count, first)
    block = pl.BlockSpec((step, rows, cols), lambda e: (first // step + e, 0, 0))
    return pl.pallas_call(
        functools.partial(sums_body, first, step),
        grid=(count // step,),
        in_specs=[SMEM, block, block],
        out_specs=pl.BlockSpec((count, cols), lambda e: (0, 0)),
        out_shape=jax.ShapeDtypeStruct((count, cols), jnp.float32),
        name="sums",
    )(mix, w, avg)


def pack_body(first, skip, ways, me_ref, mix_ref, w_ref, avg_ref, *refs):
    addends, out_refs, held_ref = refs[: -1 - ways], refs[-1 - ways : -1], refs[-1]
    me = me_ref[0]
    step, rows, cols = w_ref.shape
    width = cols // ways
    for i in range(step):
        at = pl.program_id(0) * step + i
        mix = mix_ref[first + at]
        row = pl.ds(skip + at, 1)
        total = sum(ref[row, :] for ref in addends)
        inverse = 1.0 / (total * (1.0 / (ways * rows)))
        for j in range(ways):
            cut = slice(j * width, (j + 1) * width)
            fresh = mix * w_ref[i, :, cut] + (1.0 - mix) * avg_ref[i, :, cut]
            held_ref[me ^ j] = (fresh * inverse[:, cut]).astype(jnp.bfloat16)
        for k in range(ways):
            out_refs[k][i] = held_ref[k]


def pack(me, mix, w, avg, addends, first, count, skip, ways):
    _, rows, cols = w.shape
    step = step_of(2, count, first)
    block = pl.BlockSpec((step, rows, cols), lambda e: (first // step + e, 0, 0))
    piece = (rows, cols // ways)
    return pl.pallas_call(
        functools.partial(pack_body, first, skip, ways),
        grid=(count // step,),
        in_specs=[SMEM, SMEM, block, block]
        + [pl.BlockSpec(addends[0].shape, lambda e: (0, 0))] * len(addends),
        out_specs=[pl.BlockSpec((step,) + piece, lambda e: (e, 0, 0))] * ways,
        out_shape=[jax.ShapeDtypeStruct((count,) + piece, jnp.bfloat16)] * ways,
        scratch_shapes=[pltpu.VMEM((ways,) + piece, jnp.bfloat16)],
        name="pack",
    )(me, mix, w, avg, *addends)


def unpack_body(ways, me_ref, *refs):
    out_ref = refs[-1]
    me = me_ref[0]
    step, rows, _ = refs[0].shape
    for k in range(ways):
        at = pl.multiple_of((me ^ k) * rows, rows)
        for i in range(step):
            out_ref[i, pl.ds(at, rows), :] = refs[k][i]


def unpack(me, received, whole, first, total):
    ways = len(received)
    count, rows, width = received[0].shape
    step = step_of(4, count, first)
    held = [] if whole is None else [whole]
    return pl.pallas_call(
        functools.partial(unpack_body, ways),
        grid=(count // step,),
        in_specs=[SMEM]
        + [pl.BlockSpec((step, rows, width), lambda e: (e, 0, 0))] * ways
        + [ANY] * len(held),
        out_specs=pl.BlockSpec((step, ways * rows, width), lambda e: (first // step + e, 0, 0)),
        out_shape=jax.ShapeDtypeStruct((total, ways * rows, width), jnp.bfloat16),
        input_output_aliases={1 + ways: 0} if held else {},
        name="unpack",
    )(me, *received, *held)


def swap(value, k, axis, ways):
    return lax.ppermute(value, axis, [(d, d ^ k) for d in range(ways)])


def crossings(ways):
    return list(reversed(range(1, ways)))


def doublings(ways):
    return [1 << b for b in range(ways.bit_length() - 1)]


def router_fold_body(weight_ref, gain_ref, out_ref):
    out_ref[...] = (weight_ref[...] * gain_ref[...]).astype(jnp.bfloat16)


def router_fold(weight, gain):
    full = lambda shape: pl.BlockSpec(shape, lambda: (0, 0))
    return pl.pallas_call(
        router_fold_body,
        in_specs=[full(weight.shape), full(gain.shape)],
        out_specs=full(weight.shape),
        out_shape=jax.ShapeDtypeStruct(weight.shape, jnp.bfloat16),
        name="router_fold",
    )(weight, gain)


def join_body(places, axis, me_ref, in_ref, out_ref):
    size = in_ref.shape[1 + axis]
    for i, place in enumerate(places):
        at = me_ref[0] ^ place
        if out_ref.ndim == 3:
            out_ref[at] = in_ref[i]
        elif axis == 0:
            out_ref[pl.ds(pl.multiple_of(at * size, size), size), :] = in_ref[i]
        else:
            out_ref[:, pl.ds(pl.multiple_of(at * size, size), size)] = in_ref[i]


def join(me, pieces, places, axis):
    shape = list(pieces.shape[1:])
    aligned = axis == 0 or shape[axis] % 128 == 0
    shape[axis] *= len(places)
    made = tuple(shape) if aligned else pieces.shape
    out = pl.pallas_call(
        functools.partial(join_body, places, axis),
        in_specs=[SMEM, pl.BlockSpec(pieces.shape, lambda: (0, 0, 0))],
        out_specs=pl.BlockSpec(made, lambda: (0,) * len(made)),
        out_shape=jax.ShapeDtypeStruct(made, jnp.bfloat16),
        name="join",
    )(me, pieces)
    return out if aligned else jnp.swapaxes(out, 0, 1).reshape(shape)


def gather(value, me, axis, ways, along):
    pieces, places = value[None], [0]
    for k in reversed(doublings(ways)):
        pieces = jnp.concatenate([pieces, swap(pieces, k, axis, ways)], axis=0)
        places = places + [place ^ k for place in places]
    return join(me, pieces, places, along)


def on_device(ways, banks, w_gate, avg_gate, w_up, avg_up, mix_share, router_weight, router_gain):
    experts, rows, cols = w_gate.shape
    width = cols // ways
    index = lax.axis_index("zero")
    me = jnp.reshape(index, (1,))
    my_bank = jnp.reshape(lax.axis_index("bank"), (1,))

    served, scales = [], []
    g = c = 0
    for w, avg, shares in ((w_gate, avg_gate, GATE_GROUPS), (w_up, avg_up, UP_GROUPS)):
        whole, own = None, []
        for chunks in spans(shares, experts):
            start = chunks[0][0]
            total = sums(mix_share, w, avg, start, sum(n for _, n in chunks))
            for k in doublings(ways):
                addends = [total, swap(total, k, "zero", ways)]
                total = addends[0] + addends[1]
            own.append(lax.dynamic_slice_in_dim(total, index * width, width, axis=1))
            for first, count in chunks:
                sent = pack(me, mix_share, w, avg, addends, first, count, first - start, ways)
                received = list(sent)
                for k in crossings(ways):
                    received[k] = swap(sent[k], k, "zero", ways)
                whole = unpack(me, received, whole, first, experts)
                c += 1
            g += 1
        served.append(whole)
        scales.append(jnp.concatenate(own, axis=0) / (ways * rows))

    router = router_fold(router_weight.T, router_gain[None, :])
    router = gather(router, me, "zero", ways, 1)
    router = gather(router, my_bank, "bank", banks, 0)
    return (served[0], served[1], scales[0], scales[1], router.T)


def solution(mesh):
    ways, banks = mesh.shape["zero"], mesh.shape["bank"]
    assert ways & (ways - 1) == 0 and banks & (banks - 1) == 0
    in_specs = (
        P("bank", "zero", None),
        P("bank", "zero", None),
        P("bank", "zero", None),
        P("bank", "zero", None),
        P("bank"),
        P("zero", "bank"),
        P("zero"),
    )
    out_specs = (
        P("bank", None, "zero"),
        P("bank", None, "zero"),
        P("bank", "zero"),
        P("bank", "zero"),
        P(),
    )

    def step(*args):
        def body(*local):
            return on_device(ways, banks, *local)

        local = jax.shard_map(
            body, mesh=mesh, in_specs=in_specs, out_specs=out_specs, check_vma=False
        )
        return local(*args)

    return step
```

time: 644 us -> 468 us (0.73)
  the two profiles are of different devices: /device:TPU:0 before, /device:TPU:8 now
where the time goes in v1:
time: 468 us; the launch traced here: 467 us
  waiting for transfers between devices  205 us (44%)
  starting transfers between devices  148 us (32%)
  Pallas kernels  101 us (22%)
  other arithmetic  7.09 us (2%)
  local copies, waits for them, and re-layouts  5.37 us (1%)
    ppermute x70, waiting for transfers between devices, swap(): return lax.ppermute(value, axis, [(d, d ^ k) for d in range(ways)])  205 us
    ppermute x70, starting transfers between devices, swap(): return lax.ppermute(value, axis, [(d, d ^ k) for d in range(ways)])  148 us
    pallas_call x8, Pallas kernels, pack(): pl.pallas_call(functools.partial(pack_body, first, skip, ways), grid=(cou...  44.3 us
    pallas_call x3, Pallas kernels, sums(): pl.pallas_call(functools.partial(sums_body, first, step), grid=(count //...  29.1 us
    pallas_call x8, Pallas kernels, unpack(): pl.pallas_call(functools.partial(unpack_body, ways), grid=(count // step,...  22.9 us
  transfers between devices with their start and end apart: 70, of which 28 were waited for; matrix products, arithmetic and copies ran while one was open for 1% of the time, Pallas kernels for 21%

profile of v1, /device:TPU:8, one launch (start us, length us, event | category | flops | bytes accessed | tf_op | source)
XLA Modules:
  0.0 467.1 jit_solution(10117259495729456333)
XLA Ops:
  7.5 7.7 %sums.4 = f32[8,1024]{1,0:T(8,128)} custom-call(f32[16]{0:T(128)} %mix_ref.21, f32[16,256,1024]{2,1,0:T(8,128)} %w_ref.16, f32[16,256,1024]{2,1,0:T(8,128)} %avg_ref.16), custom_call_target="tpu_custom_call" | custom-call | tf_op jit(solution)/shard_map/sums/pallas_call | solution.py:50
  17.4 13.8 %sums.5 = f32[16,1024]{1,0:T(8,128)} custom-call(f32[16]{0:T(128)} %mix_ref.21, f32[16,256,1024]{2,1,0:T(8,128)} %w_ref.21, f32[16,256,1024]{2,1,0:T(8,128)} %avg_ref.21), custom_call_target="tpu_custom_call" | custom-call | tf_op jit(solution)/shard_map/sums/pallas_call | solution.py:50
  38.3 7.7 %sums.3 = f32[8,1024]{1,0:T(8,128)} custom-call(f32[16]{0:T(128)} %mix_ref.21, f32[16,256,1024]{2,1,0:T(8,128)} %w_ref.16, f32[16,256,1024]{2,1,0:T(8,128)} %avg_ref.16), custom_call_target="tpu_custom_call" | custom-call | tf_op jit(solution)/shard_map/sums/pallas_call | solution.py:50
  53.6 5.2 %pack.11 = (bf16[4,256,128]{2,1,0:T(8,128)(2,1)}, bf16[4,256,128]{2,1,0:T(8,128)(2,1)}, bf16[4,256,128]{2,1,0:T(8,128)(2,1)}, bf16[4,256,128]{2,1,0:T(8,128)(2,1...) custom-call(s32[1]{0:T(128)} %bitcast.me_ref, ...), custom_call_target="tpu_custom_call" | custom-call | tf_op jit(solution)/shard_map/pack/pallas_call | solution.py:84
  65.1 6.1 %collective-permute-done.36.refs_1_ = f32[16,1024]{1,0:T(8,128)S(1)} collective-permute-done((f32[16,1024]{1,0:T(8,128)S(1)}, f32[16,1024]{1,0:T(8,128)S(1)}, u32[]{:S(2)}, u32[]{:S(2)}) %collective-permute-start.36) | collective-permute-done | bytes 65568 | tf_op jit(solution)/shard_map/ppermute | solution.py:125
  81.4 5.2 %pack.10 = (bf16[4,256,128]{2,1,0:T(8,128)(2,1)}, bf16[4,256,128]{2,1,0:T(8,128)(2,1)}, bf16[4,256,128]{2,1,0:T(8,128)(2,1)}, bf16[4,256,128]{2,1,0:T(8,128)(2,1...) custom-call(s32[1]{0:T(128)} %bitcast.me_ref, ...), custom_call_target="tpu_custom_call" | custom-call | tf_op jit(solution)/shard_map/pack/pallas_call | solution.py:84
  87.3 3.5 collective-permute-start.31
  94.4 13.4 %collective-permute-done.30.refs_4_ = bf16[4,256,128]{2,1,0:T(8,128)(2,1)S(1)} collective-permute-done((bf16[4,256,128]{2,1,0:T(8,128)(2,1)S(1)}, bf16[4,256,128]{2,1,0:T(8,128)(2,1)S(1)}, u32[]{:S(2)}, u32[]{:S(2)}) %collective-permute-start.30) | collective-permute-done | bytes 262176 | tf_op jit(solution)/shard_map/ppermute | solution.py:125
  107.8 2.9 collective-permute-start.21
  110.7 2.7 collective-permute-done.31.refs_5_
  114.2 3.7 collective-permute-start.22
  117.9 3.0 collective-permute-done.32.refs_6_
  121.0 17.8 %collective-permute-done.33.refs_7_ = bf16[4,256,128]{2,1,0:T(8,128)(2,1)S(1)} collective-permute-done((bf16[4,256,128]{2,1,0:T(8,128)(2,1)S(1)}, bf16[4,256,128]{2,1,0:T(8,128)(2,1)S(1)}, u32[]{:S(2)}, u32[]{:S(2)}) %collective-permute-start.33) | collective-permute-done | bytes 262176 | tf_op jit(solution)/shard_map/ppermute | solution.py:125
  139.5 3.3 collective-permute-start.25
  143.8 5.3 %pack.9 = (bf16[4,256,128]{2,1,0:T(8,128)(2,1)}, bf16[4,256,128]{2,1,0:T(8,128)(2,1)}, bf16[4,256,128]{2,1,0:T(8,128)(2,1)}, bf16[4,256,128]{2,1,0:T(8,128)(2,1)...) custom-call(s32[1]{0:T(128)} %bitcast.me_ref, ...), custom_call_target="tpu_custom_call" | custom-call | tf_op jit(solution)/shard_map/pack/pallas_call | solution.py:84
  149.7 5.3 %collective-permute-start.11 = (bf16[4,256,128]{2,1,0:T(8,128)(2,1)}, bf16[4,256,128]{2,1,0:T(8,128)(2,1)S(1)}, u32[]{:S(2)}, u32[]{:S(2)}) collective-permute-start(bf16[4,256,128]{2,1,0:T(8,128)(2,1)} %get-tuple-element.79), channel_id=1, source_target_pairs={{0,2},{1,3},{2,0},{3,1},{4,6},{5,7},{6,4},{7,5},{8,10},{9,11},{10,... | collective-permute-start | bytes 786440 | tf_op jit(solution)/shard_map/ppermute | solution.py:125
  155.0 3.5 collective-permute-done.24.refs_5_
  158.5 3.7 collective-permute-start.12
  162.2 3.7 collective-permute-done.25.refs_6_
  165.9 10.3 %collective-permute-done.26.refs_7_ = bf16[4,256,128]{2,1,0:T(8,128)(2,1)S(1)} collective-permute-done((bf16[4,256,128]{2,1,0:T(8,128)(2,1)}, bf16[4,256,128]{2,1,0:T(8,128)(2,1)S(1)}, u32[]{:S(2)}, u32[]{:S(2)}) %collective-permute-start.26) | collective-permute-done | bytes 262176 | tf_op jit(solution)/shard_map/ppermute | solution.py:125
  176.1 5.3 %pack.8 = (bf16[4,256,128]{2,1,0:T(8,128)(2,1)}, bf16[4,256,128]{2,1,0:T(8,128)(2,1)}, bf16[4,256,128]{2,1,0:T(8,128)(2,1)}, bf16[4,256,128]{2,1,0:T(8,128)(2,1)...) custom-call(s32[1]{0:T(128)} %bitcast.me_ref, ...), custom_call_target="tpu_custom_call" | custom-call | tf_op jit(solution)/shard_map/pack/pallas_call | solution.py:84
  181.5 5.3 %collective-permute-start.15 = (bf16[4,256,128]{2,1,0:T(8,128)(2,1)}, bf16[4,256,128]{2,1,0:T(8,128)(2,1)S(1)}, u32[]{:S(2)}, u32[]{:S(2)}) collective-permute-start(bf16[4,256,128]{2,1,0:T(8,128)(2,1)} %get-tuple-element.83), channel_id=1, source_target_pairs={{0,6},{1,7},{2,4},{3,5},{4,2},{5,3},{6,0},{7,1},{8,14},{9,15},{10,... | collective-permute-start | bytes 786440 | tf_op jit(solution)/shard_map/ppermute | solution.py:125
  188.4 4.6 collective-permute-done.13.refs_4_
  193.0 4.8 %collective-permute-start.4 = (bf16[4,256,128]{2,1,0:T(8,128)(2,1)}, bf16[4,256,128]{2,1,0:T(8,128)(2,1)S(1)}, u32[]{:S(2)}, u32[]{:S(2)}) collective-permute-start(bf16[4,256,128]{2,1,0:T(8,128)(2,1)} %get-tuple-element.71), channel_id=1, source_target_pairs={{0,2},{1,3},{2,0},{3,1},{4,6},{5,7},{6,4},{7,5},{8,10},{9,11},{10,... | collective-permute-start | bytes 786440 | tf_op jit(solution)/shard_map/ppermute | solution.py:125
  197.9 5.6 %collective-permute-done.14.refs_5_ = bf16[4,256,128]{2,1,0:T(8,128)(2,1)S(1)} collective-permute-done((bf16[4,256,128]{2,1,0:T(8,128)(2,1)}, bf16[4,256,128]{2,1,0:T(8,128)(2,1)S(1)}, u32[]{:S(2)}, u32[]{:S(2)}) %collective-permute-start.14) | collective-permute-done | bytes 262176 | tf_op jit(solution)/shard_map/ppermute | solution.py:125
  203.5 3.7 collective-permute-start.5
  207.2 3.7 collective-permute-done.15.refs_6_
  210.9 11.1 %collective-permute-done.16.refs_7_ = bf16[4,256,128]{2,1,0:T(8,128)(2,1)S(1)} collective-permute-done((bf16[4,256,128]{2,1,0:T(8,128)(2,1)S(1)}, bf16[4,256,128]{2,1,0:T(8,128)(2,1)S(1)}, u32[]{:S(2)}, u32[]{:S(2)}) %collective-permute-start.16) | collective-permute-done | bytes 262176 | tf_op jit(solution)/shard_map/ppermute | solution.py:125
  222.0 4.5 collective-permute-start.8
  226.5 3.9 collective-permute-start.9
  230.3 5.0 %pack.13 = (bf16[3,256,128]{2,1,0:T(8,128)(2,1)}, bf16[3,256,128]{2,1,0:T(8,128)(2,1)}, bf16[3,256,128]{2,1,0:T(8,128)(2,1)}, bf16[3,256,128]{2,1,0:T(8,128)(2,1...) custom-call(s32[1]{0:T(128)} %bitcast.me_ref, ...), custom_call_target="tpu_custom_call" | custom-call | tf_op jit(solution)/shard_map/pack/pallas_call | solution.py:84
  235.5 7.4 %collective-permute-done.6.refs_4_ = bf16[4,256,128]{2,1,0:T(8,128)(2,1)S(1)} collective-permute-done((bf16[4,256,128]{2,1,0:T(8,128)(2,1)}, bf16[4,256,128]{2,1,0:T(8,128)(2,1)S(1)}, u32[]{:S(2)}, u32[]{:S(2)}) %collective-permute-start.6) | collective-permute-done | bytes 262176 | tf_op jit(solution)/shard_map/ppermute | solution.py:125
  243.0 2.8 collective-permute-start.45
  245.7 2.8 collective-permute-done.7.refs_5_
  248.6 3.6 collective-permute-start.46
  252.2 3.7 collective-permute-done.8.refs_6_
  255.9 10.7 %collective-permute-done.9.refs_7_ = bf16[4,256,128]{2,1,0:T(8,128)(2,1)} collective-permute-done((bf16[4,256,128]{2,1,0:T(8,128)(2,1)}, bf16[4,256,128]{2,1,0:T(8,128)(2,1)}, u32[]{:S(2)}, u32[]{:S(2)}) %collective-permute-start.9) | collective-permute-done | bytes 262176 | tf_op jit(solution)/shard_map/ppermute | solution.py:125
  266.6 2.8 collective-permute-start.49
  269.5 7.8 %pack.15 = (bf16[6,256,128]{2,1,0:T(8,128)(2,1)}, bf16[6,256,128]{2,1,0:T(8,128)(2,1)}, bf16[6,256,128]{2,1,0:T(8,128)(2,1)}, bf16[6,256,128]{2,1,0:T(8,128)(2,1...) custom-call(s32[1]{0:T(128)} %bitcast.me_ref, ...), custom_call_target="tpu_custom_call" | custom-call | tf_op jit(solution)/shard_map/pack/pallas_call | solution.py:84
  278.1 3.3 collective-permute-start.59
  287.3 7.8 %pack.14 = (bf16[6,256,128]{2,1,0:T(8,128)(2,1)}, bf16[6,256,128]{2,1,0:T(8,128)(2,1)}, bf16[6,256,128]{2,1,0:T(8,128)(2,1)}, bf16[6,256,128]{2,1,0:T(8,128)(2,1...) custom-call(s32[1]{0:T(128)} %bitcast.me_ref, ...), custom_call_target="tpu_custom_call" | custom-call | tf_op jit(solution)/shard_map/pack/pallas_call | solution.py:84
  295.1 17.9 %collective-permute-done.50.refs_7_ = bf16[3,256,128]{2,1,0:T(8,128)(2,1)S(1)} collective-permute-done((bf16[3,256,128]{2,1,0:T(8,128)(2,1)S(1)}, bf16[3,256,128]{2,1,0:T(8,128)(2,1)S(1)}, u32[]{:S(2)}, u32[]{:S(2)}) %collective-permute-start.50) | collective-permute-done | bytes 196640 | tf_op jit(solution)/shard_map/ppermute | solution.py:125
  313.0 12.8 %collective-permute-start.63 = (bf16[6,256,128]{2,1,0:T(8,128)(2,1)}, bf16[6,256,128]{2,1,0:T(8,128)(2,1)S(1)}, u32[]{:S(2)}, u32[]{:S(2)}) collective-permute-start(bf16[6,256,128]{2,1,0:T(8,128)(2,1)} %get-tuple-element.131), channel_id=1, source_target_pairs={{0,6},{1,7},{2,4},{3,5},{4,2},{5,3},{6,0},{7,1},{8,14},{9,15},{10,... | collective-permute-start | bytes 1179656 | tf_op jit(solution)/shard_map/ppermute | solution.py:125
  325.8 3.4 collective-permute-start.64
  329.2 3.8 collective-permute-start.52
  333.0 12.5 %collective-permute-done.62.refs_5_ = bf16[6,256,128]{2,1,0:T(8,128)(2,1)S(1)} collective-permute-done((bf16[6,256,128]{2,1,0:T(8,128)(2,1)}, bf16[6,256,128]{2,1,0:T(8,128)(2,1)S(1)}, u32[]{:S(2)}, u32[]{:S(2)}) %collective-permute-start.62) | collective-permute-done | bytes 393248 | tf_op jit(solution)/shard_map/ppermute | solution.py:125
  345.5 5.0 %collective-permute-start.53 = (bf16[6,256,128]{2,1,0:T(8,128)(2,1)}, bf16[6,256,128]{2,1,0:T(8,128)(2,1)}, u32[]{:S(2)}, u32[]{:S(2)}) collective-permute-start(bf16[6,256,128]{2,1,0:T(8,128)(2,1)} %get-tuple-element.120), channel_id=1, source_target_pairs={{0,3},{1,2},{2,1},{3,0},{4,7},{5,6},{6,5},{7,4},{8,11},{9,10},{10,... | collective-permute-start | bytes 1179656 | tf_op jit(solution)/shard_map/ppermute | solution.py:125
  350.5 6.5 %collective-permute-done.63.refs_6_ = bf16[6,256,128]{2,1,0:T(8,128)(2,1)S(1)} collective-permute-done((bf16[6,256,128]{2,1,0:T(8,128)(2,1)}, bf16[6,256,128]{2,1,0:T(8,128)(2,1)S(1)}, u32[]{:S(2)}, u32[]{:S(2)}) %collective-permute-start.63) | collective-permute-done | bytes 393248 | tf_op jit(solution)/shard_map/ppermute | solution.py:125
  357.0 15.1 %collective-permute-done.64.refs_7_ = bf16[6,256,128]{2,1,0:T(8,128)(2,1)S(1)} collective-permute-done((bf16[6,256,128]{2,1,0:T(8,128)(2,1)}, bf16[6,256,128]{2,1,0:T(8,128)(2,1)S(1)}, u32[]{:S(2)}, u32[]{:S(2)}) %collective-permute-start.64) | collective-permute-done | bytes 393248 | tf_op jit(solution)/shard_map/ppermute | solution.py:125
  372.1 17.3 %collective-permute-start.56 = (bf16[6,256,128]{2,1,0:T(8,128)(2,1)}, bf16[6,256,128]{2,1,0:T(8,128)(2,1)}, u32[]{:S(2)}, u32[]{:S(2)}) collective-permute-start(bf16[6,256,128]{2,1,0:T(8,128)(2,1)} %get-tuple-element.123), channel_id=1, source_target_pairs={{0,6},{1,7},{2,4},{3,5},{4,2},{5,3},{6,0},{7,1},{8,14},{9,15},{10,... | collective-permute-start | bytes 1179656 | tf_op jit(solution)/shard_map/ppermute | solution.py:125
  392.8 2.9 collective-permute-start.39
  395.7 10.9 %collective-permute-done.54.refs_4_ = bf16[6,256,128]{2,1,0:T(8,128)(2,1)} collective-permute-done((bf16[6,256,128]{2,1,0:T(8,128)(2,1)}, bf16[6,256,128]{2,1,0:T(8,128)(2,1)}, u32[]{:S(2)}, u32[]{:S(2)}) %collective-permute-start.54) | collective-permute-done | bytes 393248 | tf_op jit(solution)/shard_map/ppermute | solution.py:125
  406.6 3.4 collective-permute-start.40
  410.0 7.0 %collective-permute-done.55.refs_5_ = bf16[6,256,128]{2,1,0:T(8,128)(2,1)} collective-permute-done((bf16[6,256,128]{2,1,0:T(8,128)(2,1)}, bf16[6,256,128]{2,1,0:T(8,128)(2,1)}, u32[]{:S(2)}, u32[]{:S(2)}) %collective-permute-start.55) | collective-permute-done | bytes 393248 | tf_op jit(solution)/shard_map/ppermute | solution.py:125
  417.0 4.4 collective-permute-start.41
  421.4 8.9 %collective-permute-done.56.refs_6_ = bf16[6,256,128]{2,1,0:T(8,128)(2,1)} collective-permute-done((bf16[6,256,128]{2,1,0:T(8,128)(2,1)}, bf16[6,256,128]{2,1,0:T(8,128)(2,1)}, u32[]{:S(2)}, u32[]{:S(2)}) %collective-permute-start.56) | collective-permute-done | bytes 393248 | tf_op jit(solution)/shard_map/ppermute | solution.py:125
  430.8 8.5 %collective-permute-done.57.refs_7_ = bf16[6,256,128]{2,1,0:T(8,128)(2,1)} collective-permute-done((bf16[6,256,128]{2,1,0:T(8,128)(2,1)}, bf16[6,256,128]{2,1,0:T(8,128)(2,1)}, u32[]{:S(2)}, u32[]{:S(2)}) %collective-permute-start.57) | collective-permute-done | bytes 393248 | tf_op jit(solution)/shard_map/ppermute | solution.py:125
  443.5 3.0 unpack.8.refs_8_
  446.4 3.0 unpack.9.refs_8_
  449.4 3.0 unpack.10.refs_8_
  452.4 3.0 unpack.11
  455.4 3.2 unpack.12.refs_8_
  458.6 3.2 unpack.13.refs_8_
  461.9 2.7 unpack.14.refs_8_
  (231 shorter events, 66.3 us)
Async XLA Ops:
  7.4 9.7 %collective-permute-start.66 = (bf16[2,16,256]{2,1,0:T(8,128)(2,1)S(1)}, bf16[2,16,256]{2,1,0:T(8,128)(2,1)S(1)}, u32[]{:S(2)}, u32[]{:S(2)}) collective-permute-start(bf16[2,16,256]{2,1,0:T(8,128)(2,1)S(1)} %pad_maximum_fusion.4), channel_id=1, source_target_pairs={{0,2},{1,3},{2,0},{3,1},{4,6},{5,7},{6,4},{7,5},{8,10},{9,11},{10,... | collective-permute-start | bytes 49160 | tf_op jit(solution)/shard_map/ppermute | solution.py:125
  15.2 17.8 %collective-permute-start.17 = (f32[8,1024]{1,0:T(8,128)}, f32[8,1024]{1,0:T(8,128)S(1)}, u32[]{:S(2)}, u32[]{:S(2)}) collective-permute-start(f32[8,1024]{1,0:T(8,128)} %sums.4), channel_id=1, source_target_pairs={{0,1},{1,0},{2,3},{3,2},{4,5},{5,4},{6,7},{7,6},{8,9},{9,8},{10,11... | collective-permute-start | bytes 98312 | tf_op jit(solution)/shard_map/ppermute | solution.py:125
  17.1 17.5 %collective-permute-start.67 = (bf16[4,16,256]{2,1,0:T(8,128)(2,1)S(1)}, bf16[4,16,256]{2,1,0:T(8,128)(2,1)S(1)}, u32[]{:S(2)}, u32[]{:S(2)}) collective-permute-start(bf16[4,16,256]{2,1,0:T(8,128)(2,1)S(1)} %pad_maximum_fusion.3), channel_id=1, source_target_pairs={{0,1},{1,0},{2,3},{3,2},{4,5},{5,4},{6,7},{7,6},{8,9},{9,8},{10,11... | collective-permute-start | bytes 98312 | tf_op jit(solution)/shard_map/ppermute | solution.py:125
  31.1 20.1 %collective-permute-start.34 = (f32[16,1024]{1,0:T(8,128)}, f32[16,1024]{1,0:T(8,128)S(1)}, u32[]{:S(2)}, u32[]{:S(2)}) collective-permute-start(f32[16,1024]{1,0:T(8,128)} %sums.5), channel_id=1, source_target_pairs={{0,1},{1,0},{2,3},{3,2},{4,5},{5,4},{6,7},{7,6},{8,9},{9,8},{10,11... | collective-permute-start | bytes 196616 | tf_op jit(solution)/shard_map/ppermute | solution.py:125
  33.0 13.4 %collective-permute-start.18 = (f32[8,1024]{1,0:T(8,128)S(1)}, f32[8,1024]{1,0:T(8,128)S(1)}, u32[]{:S(2)}, u32[]{:S(2)}) collective-permute-start(f32[8,1024]{1,0:T(8,128)S(1)} %add.34), channel_id=1, source_target_pairs={{0,2},{1,3},{2,0},{3,1},{4,6},{5,7},{6,4},{7,5},{8,10},{9,11},{10,... | collective-permute-start | bytes 98312 | tf_op jit(solution)/shard_map/ppermute | solution.py:125
  36.8 23.1 %collective-permute-start.68 = (bf16[1,16,2048]{2,1,0:T(8,128)(2,1)}, bf16[1,16,2048]{2,1,0:T(8,128)(2,1)S(1)}, u32[]{:S(2)}, u32[]{:S(2)}) collective-permute-start(bf16[1,16,2048]{2,1,0:T(8,128)(2,1)} %bitcast.7), channel_id=1, source_target_pairs={{0,16},{8,24},{16,0},{24,8},{1,17},{9,25},{17,1},{25,9},{2,18},{10... | collective-permute-start | bytes 196616 | tf_op jit(solution)/shard_map/ppermute | solution.py:125
  50.8 11.6 %collective-permute-start.1 = (f32[8,1024]{1,0:T(8,128)S(1)}, f32[8,1024]{1,0:T(8,128)S(1)}, u32[]{:S(2)}, u32[]{:S(2)}) collective-permute-start(f32[8,1024]{1,0:T(8,128)S(1)} %add.32), channel_id=1, source_target_pairs={{0,2},{1,3},{2,0},{3,1},{4,6},{5,7},{6,4},{7,5},{8,10},{9,11},{10,... | collective-permute-start | bytes 98312 | tf_op jit(solution)/shard_map/ppermute | solution.py:125
  51.3 11.0 %collective-permute-start.35 = (f32[16,1024]{1,0:T(8,128)S(1)}, f32[16,1024]{1,0:T(8,128)S(1)}, u32[]{:S(2)}, u32[]{:S(2)}) collective-permute-start(f32[16,1024]{1,0:T(8,128)S(1)} %add.36), channel_id=1, source_target_pairs={{0,2},{1,3},{2,0},{3,1},{4,6},{5,7},{6,4},{7,5},{8,10},{9,11},{10,... | collective-permute-start | bytes 196616 | tf_op jit(solution)/shard_map/ppermute | solution.py:125
  58.8 32.0 %collective-permute-start.27 = (bf16[4,256,128]{2,1,0:T(8,128)(2,1)}, bf16[4,256,128]{2,1,0:T(8,128)(2,1)S(1)}, u32[]{:S(2)}, u32[]{:S(2)}) collective-permute-start(bf16[4,256,128]{2,1,0:T(8,128)(2,1)} %get-tuple-element.94), channel_id=1, source_target_pairs={{0,1},{1,0},{2,3},{3,2},{4,5},{5,4},{6,7},{7,6},{8,9},{9,8},{10,11... | collective-permute-start | bytes 786440 | tf_op jit(solution)/shard_map/ppermute | solution.py:125
  59.4 31.5 %collective-permute-start.28 = (bf16[4,256,128]{2,1,0:T(8,128)(2,1)}, bf16[4,256,128]{2,1,0:T(8,128)(2,1)S(1)}, u32[]{:S(2)}, u32[]{:S(2)}) collective-permute-start(bf16[4,256,128]{2,1,0:T(8,128)(2,1)} %get-tuple-element.95), channel_id=1, source_target_pairs={{0,2},{1,3},{2,0},{3,1},{4,6},{5,7},{6,4},{7,5},{8,10},{9,11},{10,... | collective-permute-start | bytes 786440 | tf_op jit(solution)/shard_map/ppermute | solution.py:125
  59.9 32.7 %collective-permute-start.29 = (bf16[4,256,128]{2,1,0:T(8,128)(2,1)}, bf16[4,256,128]{2,1,0:T(8,128)(2,1)S(1)}, u32[]{:S(2)}, u32[]{:S(2)}) collective-permute-start(bf16[4,256,128]{2,1,0:T(8,128)(2,1)} %get-tuple-element.96), channel_id=1, source_target_pairs={{0,3},{1,2},{2,1},{3,0},{4,7},{5,6},{6,5},{7,4},{8,11},{9,10},{10,... | collective-permute-start | bytes 786440 | tf_op jit(solution)/shard_map/ppermute | solution.py:125
  62.3 15.6 %collective-permute-start.69 = (bf16[2,16,2048]{2,1,0:T(8,128)(2,1)S(1)}, bf16[2,16,2048]{2,1,0:T(8,128)(2,1)S(1)}, u32[]{:S(2)}, u32[]{:S(2)}) collective-permute-start(bf16[2,16,2048]{2,1,0:T(8,128)(2,1)S(1)} %pad_maximum_fusion.1), channel_id=1, source_target_pairs={{0,8},{8,0},{16,24},{24,16},{1,9},{9,1},{17,25},{25,17},{2,10},{10... | collective-permute-start | bytes 393224 | tf_op jit(solution)/shard_map/ppermute | solution.py:125
  62.5 8.7 %collective-permute-start.36 = (f32[16,1024]{1,0:T(8,128)S(1)}, f32[16,1024]{1,0:T(8,128)S(1)}, u32[]{:S(2)}, u32[]{:S(2)}) collective-permute-start(f32[16,1024]{1,0:T(8,128)S(1)} %add.37.refs_0_), channel_id=1, source_target_pairs={{0,4},{1,5},{2,6},{3,7},{4,0},{5,1},{6,2},{7,3},{8,12},{9,13},{10,... | collective-permute-start | bytes 196616 | tf_op jit(solution)/shard_map/ppermute | solution.py:125
  80.6 27.2 %collective-permute-start.30 = (bf16[4,256,128]{2,1,0:T(8,128)(2,1)S(1)}, bf16[4,256,128]{2,1,0:T(8,128)(2,1)S(1)}, u32[]{:S(2)}, u32[]{:S(2)}) collective-permute-start(bf16[4,256,128]{2,1,0:T(8,128)(2,1)S(1)} %copy-done.56), channel_id=1, source_target_pairs={{0,4},{1,5},{2,6},{3,7},{4,0},{5,1},{6,2},{7,3},{8,12},{9,13},{10,... | collective-permute-start | bytes 786440 | tf_op jit(solution)/shard_map/ppermute | solution.py:125
  87.3 26.1 %collective-permute-start.31 = (bf16[4,256,128]{2,1,0:T(8,128)(2,1)S(1)}, bf16[4,256,128]{2,1,0:T(8,128)(2,1)S(1)}, u32[]{:S(2)}, u32[]{:S(2)}) collective-permute-start(bf16[4,256,128]{2,1,0:T(8,128)(2,1)S(1)} %copy-done.55), channel_id=1, source_target_pairs={{0,5},{1,4},{2,7},{3,6},{4,1},{5,0},{6,3},{7,2},{8,13},{9,12},{10,... | collective-permute-start | bytes 786440 | tf_op jit(solution)/shard_map/ppermute | solution.py:125
  90.8 30.2 %collective-permute-start.32 = (bf16[4,256,128]{2,1,0:T(8,128)(2,1)S(1)}, bf16[4,256,128]{2,1,0:T(8,128)(2,1)S(1)}, u32[]{:S(2)}, u32[]{:S(2)}) collective-permute-start(bf16[4,256,128]{2,1,0:T(8,128)(2,1)S(1)} %copy-done.54), channel_id=1, source_target_pairs={{0,6},{1,7},{2,4},{3,5},{4,2},{5,3},{6,0},{7,1},{8,14},{9,15},{10,... | collective-permute-start | bytes 786440 | tf_op jit(solution)/shard_map/ppermute | solution.py:125
  90.9 47.8 %collective-permute-start.33 = (bf16[4,256,128]{2,1,0:T(8,128)(2,1)S(1)}, bf16[4,256,128]{2,1,0:T(8,128)(2,1)S(1)}, u32[]{:S(2)}, u32[]{:S(2)}) collective-permute-start(bf16[4,256,128]{2,1,0:T(8,128)(2,1)S(1)} %copy-done.53), channel_id=1, source_target_pairs={{0,7},{1,6},{2,5},{3,4},{4,3},{5,2},{6,1},{7,0},{8,15},{9,14},{10,... | collective-permute-start | bytes 786440 | tf_op jit(solution)/shard_map/ppermute | solution.py:125
  92.5 46.9 %collective-permute-start.20 = (bf16[4,256,128]{2,1,0:T(8,128)(2,1)}, bf16[4,256,128]{2,1,0:T(8,128)(2,1)}, u32[]{:S(2)}, u32[]{:S(2)}) collective-permute-start(bf16[4,256,128]{2,1,0:T(8,128)(2,1)} %get-tuple-element.86), channel_id=1, source_target_pairs={{0,1},{1,0},{2,3},{3,2},{4,5},{5,4},{6,7},{7,6},{8,9},{9,8},{10,11... | collective-permute-start | bytes 786440 | tf_op jit(solution)/shard_map/ppermute | solution.py:125
  107.8 35.0 %collective-permute-start.21 = (bf16[4,256,128]{2,1,0:T(8,128)(2,1)}, bf16[4,256,128]{2,1,0:T(8,128)(2,1)}, u32[]{:S(2)}, u32[]{:S(2)}) collective-permute-start(bf16[4,256,128]{2,1,0:T(8,128)(2,1)} %get-tuple-element.87), channel_id=1, source_target_pairs={{0,2},{1,3},{2,0},{3,1},{4,6},{5,7},{6,4},{7,5},{8,10},{9,11},{10,... | collective-permute-start | bytes 786440 | tf_op jit(solution)/shard_map/ppermute | solution.py:125
  114.2 34.9 %collective-permute-start.22 = (bf16[4,256,128]{2,1,0:T(8,128)(2,1)}, bf16[4,256,128]{2,1,0:T(8,128)(2,1)S(1)}, u32[]{:S(2)}, u32[]{:S(2)}) collective-permute-start(bf16[4,256,128]{2,1,0:T(8,128)(2,1)} %get-tuple-element.88), channel_id=1, source_target_pairs={{0,3},{1,2},{2,1},{3,0},{4,7},{5,6},{6,5},{7,4},{8,11},{9,10},{10,... | collective-permute-start | bytes 786440 | tf_op jit(solution)/shard_map/ppermute | solution.py:125
  121.0 28.8 %collective-permute-start.23 = (bf16[4,256,128]{2,1,0:T(8,128)(2,1)}, bf16[4,256,128]{2,1,0:T(8,128)(2,1)S(1)}, u32[]{:S(2)}, u32[]{:S(2)}) collective-permute-start(bf16[4,256,128]{2,1,0:T(8,128)(2,1)} %get-tuple-element.89), channel_id=1, source_target_pairs={{0,4},{1,5},{2,6},{3,7},{4,0},{5,1},{6,2},{7,3},{8,12},{9,13},{10,... | collective-permute-start | bytes 786440 | tf_op jit(solution)/shard_map/ppermute | solution.py:125
  139.4 19.1 %collective-permute-start.24 = (bf16[4,256,128]{2,1,0:T(8,128)(2,1)}, bf16[4,256,128]{2,1,0:T(8,128)(2,1)S(1)}, u32[]{:S(2)}, u32[]{:S(2)}) collective-permute-start(bf16[4,256,128]{2,1,0:T(8,128)(2,1)} %get-tuple-element.90), channel_id=1, source_target_pairs={{0,5},{1,4},{2,7},{3,6},{4,1},{5,0},{6,3},{7,2},{8,13},{9,12},{10,... | collective-permute-start | bytes 786440 | tf_op jit(solution)/shard_map/ppermute | solution.py:125
  139.5 26.4 %collective-permute-start.25 = (bf16[4,256,128]{2,1,0:T(8,128)(2,1)}, bf16[4,256,128]{2,1,0:T(8,128)(2,1)S(1)}, u32[]{:S(2)}, u32[]{:S(2)}) collective-permute-start(bf16[4,256,128]{2,1,0:T(8,128)(2,1)} %get-tuple-element.91), channel_id=1, source_target_pairs={{0,6},{1,7},{2,4},{3,5},{4,2},{5,3},{6,0},{7,1},{8,14},{9,15},{10,... | collective-permute-start | bytes 786440 | tf_op jit(solution)/shard_map/ppermute | solution.py:125
  142.7 33.4 %collective-permute-start.26 = (bf16[4,256,128]{2,1,0:T(8,128)(2,1)}, bf16[4,256,128]{2,1,0:T(8,128)(2,1)S(1)}, u32[]{:S(2)}, u32[]{:S(2)}) collective-permute-start(bf16[4,256,128]{2,1,0:T(8,128)(2,1)} %get-tuple-element.92), channel_id=1, source_target_pairs={{0,7},{1,6},{2,5},{3,4},{4,3},{5,2},{6,1},{7,0},{8,15},{9,14},{10,... | collective-permute-start | bytes 786440 | tf_op jit(solution)/shard_map/ppermute | solution.py:125
  149.1 32.4 %collective-permute-start.10 = (bf16[4,256,128]{2,1,0:T(8,128)(2,1)}, bf16[4,256,128]{2,1,0:T(8,128)(2,1)S(1)}, u32[]{:S(2)}, u32[]{:S(2)}) collective-permute-start(bf16[4,256,128]{2,1,0:T(8,128)(2,1)} %get-tuple-element.78), channel_id=1, source_target_pairs={{0,1},{1,0},{2,3},{3,2},{4,5},{5,4},{6,7},{7,6},{8,9},{9,8},{10,11... | collective-permute-start | bytes 786440 | tf_op jit(solution)/shard_map/ppermute | solution.py:125
  149.7 37.1 %collective-permute-start.11 = (bf16[4,256,128]{2,1,0:T(8,128)(2,1)}, bf16[4,256,128]{2,1,0:T(8,128)(2,1)S(1)}, u32[]{:S(2)}, u32[]{:S(2)}) collective-permute-start(bf16[4,256,128]{2,1,0:T(8,128)(2,1)} %get-tuple-element.79), channel_id=1, source_target_pairs={{0,2},{1,3},{2,0},{3,1},{4,6},{5,7},{6,4},{7,5},{8,10},{9,11},{10,... | collective-permute-start | bytes 786440 | tf_op jit(solution)/shard_map/ppermute | solution.py:125
  158.5 29.4 %collective-permute-start.12 = (bf16[4,256,128]{2,1,0:T(8,128)(2,1)}, bf16[4,256,128]{2,1,0:T(8,128)(2,1)S(1)}, u32[]{:S(2)}, u32[]{:S(2)}) collective-permute-start(bf16[4,256,128]{2,1,0:T(8,128)(2,1)} %get-tuple-element.80), channel_id=1, source_target_pairs={{0,3},{1,2},{2,1},{3,0},{4,7},{5,6},{6,5},{7,4},{8,11},{9,10},{10,... | collective-permute-start | bytes 786440 | tf_op jit(solution)/shard_map/ppermute | solution.py:125
  165.9 27.2 %collective-permute-start.13 = (bf16[4,256,128]{2,1,0:T(8,128)(2,1)}, bf16[4,256,128]{2,1,0:T(8,128)(2,1)S(1)}, u32[]{:S(2)}, u32[]{:S(2)}) collective-permute-start(bf16[4,256,128]{2,1,0:T(8,128)(2,1)} %get-tuple-element.81), channel_id=1, source_target_pairs={{0,4},{1,5},{2,6},{3,7},{4,0},{5,1},{6,2},{7,3},{8,12},{9,13},{10,... | collective-permute-start | bytes 786440 | tf_op jit(solution)/shard_map/ppermute | solution.py:125
  176.1 27.4 %collective-permute-start.14 = (bf16[4,256,128]{2,1,0:T(8,128)(2,1)}, bf16[4,256,128]{2,1,0:T(8,128)(2,1)S(1)}, u32[]{:S(2)}, u32[]{:S(2)}) collective-permute-start(bf16[4,256,128]{2,1,0:T(8,128)(2,1)} %get-tuple-element.82), channel_id=1, source_target_pairs={{0,5},{1,4},{2,7},{3,6},{4,1},{5,0},{6,3},{7,2},{8,13},{9,12},{10,... | collective-permute-start | bytes 786440 | tf_op jit(solution)/shard_map/ppermute | solution.py:125
  181.5 29.3 %collective-permute-start.15 = (bf16[4,256,128]{2,1,0:T(8,128)(2,1)}, bf16[4,256,128]{2,1,0:T(8,128)(2,1)S(1)}, u32[]{:S(2)}, u32[]{:S(2)}) collective-permute-start(bf16[4,256,128]{2,1,0:T(8,128)(2,1)} %get-tuple-element.83), channel_id=1, source_target_pairs={{0,6},{1,7},{2,4},{3,5},{4,2},{5,3},{6,0},{7,1},{8,14},{9,15},{10,... | collective-permute-start | bytes 786440 | tf_op jit(solution)/shard_map/ppermute | solution.py:125
  186.9 35.1 %collective-permute-start.16 = (bf16[4,256,128]{2,1,0:T(8,128)(2,1)S(1)}, bf16[4,256,128]{2,1,0:T(8,128)(2,1)S(1)}, u32[]{:S(2)}, u32[]{:S(2)}) collective-permute-start(bf16[4,256,128]{2,1,0:T(8,128)(2,1)S(1)} %copy-done.57), channel_id=1, source_target_pairs={{0,7},{1,6},{2,5},{3,4},{4,3},{5,2},{6,1},{7,0},{8,15},{9,14},{10,... | collective-permute-start | bytes 786440 | tf_op jit(solution)/shard_map/ppermute | solution.py:125
  187.9 34.0 %collective-permute-start.3 = (bf16[4,256,128]{2,1,0:T(8,128)(2,1)}, bf16[4,256,128]{2,1,0:T(8,128)(2,1)S(1)}, u32[]{:S(2)}, u32[]{:S(2)}) collective-permute-start(bf16[4,256,128]{2,1,0:T(8,128)(2,1)} %get-tuple-element.70), channel_id=1, source_target_pairs={{0,1},{1,0},{2,3},{3,2},{4,5},{5,4},{6,7},{7,6},{8,9},{9,8},{10,11... | collective-permute-start | bytes 786440 | tf_op jit(solution)/shard_map/ppermute | solution.py:125
  193.0 33.4 %collective-permute-start.4 = (bf16[4,256,128]{2,1,0:T(8,128)(2,1)}, bf16[4,256,128]{2,1,0:T(8,128)(2,1)S(1)}, u32[]{:S(2)}, u32[]{:S(2)}) collective-permute-start(bf16[4,256,128]{2,1,0:T(8,128)(2,1)} %get-tuple-element.71), channel_id=1, source_target_pairs={{0,2},{1,3},{2,0},{3,1},{4,6},{5,7},{6,4},{7,5},{8,10},{9,11},{10,... | collective-permute-start | bytes 786440 | tf_op jit(solution)/shard_map/ppermute | solution.py:125
  203.5 31.9 %collective-permute-start.5 = (bf16[4,256,128]{2,1,0:T(8,128)(2,1)}, bf16[4,256,128]{2,1,0:T(8,128)(2,1)S(1)}, u32[]{:S(2)}, u32[]{:S(2)}) collective-permute-start(bf16[4,256,128]{2,1,0:T(8,128)(2,1)} %get-tuple-element.72), channel_id=1, source_target_pairs={{0,3},{1,2},{2,1},{3,0},{4,7},{5,6},{6,5},{7,4},{8,11},{9,10},{10,... | collective-permute-start | bytes 786440 | tf_op jit(solution)/shard_map/ppermute | solution.py:125
  210.9 32.1 %collective-permute-start.6 = (bf16[4,256,128]{2,1,0:T(8,128)(2,1)}, bf16[4,256,128]{2,1,0:T(8,128)(2,1)S(1)}, u32[]{:S(2)}, u32[]{:S(2)}) collective-permute-start(bf16[4,256,128]{2,1,0:T(8,128)(2,1)} %get-tuple-element.73), channel_id=1, source_target_pairs={{0,4},{1,5},{2,6},{3,7},{4,0},{5,1},{6,2},{7,3},{8,12},{9,13},{10,... | collective-permute-start | bytes 786440 | tf_op jit(solution)/shard_map/ppermute | solution.py:125
  222.0 26.6 %collective-permute-start.7 = (bf16[4,256,128]{2,1,0:T(8,128)(2,1)}, bf16[4,256,128]{2,1,0:T(8,128)(2,1)S(1)}, u32[]{:S(2)}, u32[]{:S(2)}) collective-permute-start(bf16[4,256,128]{2,1,0:T(8,128)(2,1)} %get-tuple-element.74), channel_id=1, source_target_pairs={{0,5},{1,4},{2,7},{3,6},{4,1},{5,0},{6,3},{7,2},{8,13},{9,12},{10,... | collective-permute-start | bytes 786440 | tf_op jit(solution)/shard_map/ppermute | solution.py:125
  222.0 33.9 %collective-permute-start.8 = (bf16[4,256,128]{2,1,0:T(8,128)(2,1)}, bf16[4,256,128]{2,1,0:T(8,128)(2,1)}, u32[]{:S(2)}, u32[]{:S(2)}) collective-permute-start(bf16[4,256,128]{2,1,0:T(8,128)(2,1)} %get-tuple-element.75), channel_id=1, source_target_pairs={{0,6},{1,7},{2,4},{3,5},{4,2},{5,3},{6,0},{7,1},{8,14},{9,15},{10,... | collective-permute-start | bytes 786440 | tf_op jit(solution)/shard_map/ppermute | solution.py:125
  226.5 40.1 %collective-permute-start.9 = (bf16[4,256,128]{2,1,0:T(8,128)(2,1)}, bf16[4,256,128]{2,1,0:T(8,128)(2,1)}, u32[]{:S(2)}, u32[]{:S(2)}) collective-permute-start(bf16[4,256,128]{2,1,0:T(8,128)(2,1)} %get-tuple-element.76), channel_id=1, source_target_pairs={{0,7},{1,6},{2,5},{3,4},{4,3},{5,2},{6,1},{7,0},{8,15},{9,14},{10,... | collective-permute-start | bytes 786440 | tf_op jit(solution)/shard_map/ppermute | solution.py:125
  235.4 31.2 %collective-permute-start.44 = (bf16[3,256,128]{2,1,0:T(8,128)(2,1)}, bf16[3,256,128]{2,1,0:T(8,128)(2,1)S(1)}, u32[]{:S(2)}, u32[]{:S(2)}) collective-permute-start(bf16[3,256,128]{2,1,0:T(8,128)(2,1)} %get-tuple-element.110), channel_id=1, source_target_pairs={{0,1},{1,0},{2,3},{3,2},{4,5},{5,4},{6,7},{7,6},{8,9},{9,8},{10,11... | collective-permute-start | bytes 589832 | tf_op jit(solution)/shard_map/ppermute | solution.py:125
  243.0 34.4 %collective-permute-start.45 = (bf16[3,256,128]{2,1,0:T(8,128)(2,1)}, bf16[3,256,128]{2,1,0:T(8,128)(2,1)S(1)}, u32[]{:S(2)}, u32[]{:S(2)}) collective-permute-start(bf16[3,256,128]{2,1,0:T(8,128)(2,1)} %get-tuple-element.111), channel_id=1, source_target_pairs={{0,2},{1,3},{2,0},{3,1},{4,6},{5,7},{6,4},{7,5},{8,10},{9,11},{10,... | collective-permute-start | bytes 589832 | tf_op jit(solution)/shard_map/ppermute | solution.py:125
  248.6 28.9 %collective-permute-start.46 = (bf16[3,256,128]{2,1,0:T(8,128)(2,1)}, bf16[3,256,128]{2,1,0:T(8,128)(2,1)S(1)}, u32[]{:S(2)}, u32[]{:S(2)}) collective-permute-start(bf16[3,256,128]{2,1,0:T(8,128)(2,1)} %get-tuple-element.112), channel_id=1, source_target_pairs={{0,3},{1,2},{2,1},{3,0},{4,7},{5,6},{6,5},{7,4},{8,11},{9,10},{10,... | collective-permute-start | bytes 589832 | tf_op jit(solution)/shard_map/ppermute | solution.py:125
  255.9 25.6 %collective-permute-start.47 = (bf16[3,256,128]{2,1,0:T(8,128)(2,1)}, bf16[3,256,128]{2,1,0:T(8,128)(2,1)S(1)}, u32[]{:S(2)}, u32[]{:S(2)}) collective-permute-start(bf16[3,256,128]{2,1,0:T(8,128)(2,1)} %get-tuple-element.113), channel_id=1, source_target_pairs={{0,4},{1,5},{2,6},{3,7},{4,0},{5,1},{6,2},{7,3},{8,12},{9,13},{10,... | collective-permute-start | bytes 589832 | tf_op jit(solution)/shard_map/ppermute | solution.py:125
  266.6 17.0 %collective-permute-start.48 = (bf16[3,256,128]{2,1,0:T(8,128)(2,1)}, bf16[3,256,128]{2,1,0:T(8,128)(2,1)S(1)}, u32[]{:S(2)}, u32[]{:S(2)}) collective-permute-start(bf16[3,256,128]{2,1,0:T(8,128)(2,1)} %get-tuple-element.114), channel_id=1, source_target_pairs={{0,5},{1,4},{2,7},{3,6},{4,1},{5,0},{6,3},{7,2},{8,13},{9,12},{10,... | collective-permute-start | bytes 589832 | tf_op jit(solution)/shard_map/ppermute | solution.py:125
  266.6 18.9 %collective-permute-start.49 = (bf16[3,256,128]{2,1,0:T(8,128)(2,1)}, bf16[3,256,128]{2,1,0:T(8,128)(2,1)S(1)}, u32[]{:S(2)}, u32[]{:S(2)}) collective-permute-start(bf16[3,256,128]{2,1,0:T(8,128)(2,1)} %get-tuple-element.115), channel_id=1, source_target_pairs={{0,6},{1,7},{2,4},{3,5},{4,2},{5,3},{6,0},{7,1},{8,14},{9,15},{10,... | collective-permute-start | bytes 589832 | tf_op jit(solution)/shard_map/ppermute | solution.py:125
  277.4 35.7 %collective-permute-start.58 = (bf16[6,256,128]{2,1,0:T(8,128)(2,1)}, bf16[6,256,128]{2,1,0:T(8,128)(2,1)S(1)}, u32[]{:S(2)}, u32[]{:S(2)}) collective-permute-start(bf16[6,256,128]{2,1,0:T(8,128)(2,1)} %get-tuple-element.126), channel_id=1, source_target_pairs={{0,1},{1,0},{2,3},{3,2},{4,5},{5,4},{6,7},{7,6},{8,9},{9,8},{10,11... | collective-permute-start | bytes 1179656 | tf_op jit(solution)/shard_map/ppermute | solution.py:125
  278.1 47.7 %collective-permute-start.59 = (bf16[6,256,128]{2,1,0:T(8,128)(2,1)}, bf16[6,256,128]{2,1,0:T(8,128)(2,1)S(1)}, u32[]{:S(2)}, u32[]{:S(2)}) collective-permute-start(bf16[6,256,128]{2,1,0:T(8,128)(2,1)} %get-tuple-element.127), channel_id=1, source_target_pairs={{0,2},{1,3},{2,0},{3,1},{4,6},{5,7},{6,4},{7,5},{8,10},{9,11},{10,... | collective-permute-start | bytes 1179656 | tf_op jit(solution)/shard_map/ppermute | solution.py:125
  282.2 47.0 %collective-permute-start.60 = (bf16[6,256,128]{2,1,0:T(8,128)(2,1)}, bf16[6,256,128]{2,1,0:T(8,128)(2,1)S(1)}, u32[]{:S(2)}, u32[]{:S(2)}) collective-permute-start(bf16[6,256,128]{2,1,0:T(8,128)(2,1)} %get-tuple-element.128), channel_id=1, source_target_pairs={{0,3},{1,2},{2,1},{3,0},{4,7},{5,6},{6,5},{7,4},{8,11},{9,10},{10,... | collective-permute-start | bytes 1179656 | tf_op jit(solution)/shard_map/ppermute | solution.py:125
  283.6 45.6 %collective-permute-start.61 = (bf16[6,256,128]{2,1,0:T(8,128)(2,1)}, bf16[6,256,128]{2,1,0:T(8,128)(2,1)S(1)}, u32[]{:S(2)}, u32[]{:S(2)}) collective-permute-start(bf16[6,256,128]{2,1,0:T(8,128)(2,1)} %get-tuple-element.129), channel_id=1, source_target_pairs={{0,4},{1,5},{2,6},{3,7},{4,0},{5,1},{6,2},{7,3},{8,12},{9,13},{10,... | collective-permute-start | bytes 1179656 | tf_op jit(solution)/shard_map/ppermute | solution.py:125
  285.6 27.4 %collective-permute-start.50 = (bf16[3,256,128]{2,1,0:T(8,128)(2,1)S(1)}, bf16[3,256,128]{2,1,0:T(8,128)(2,1)S(1)}, u32[]{:S(2)}, u32[]{:S(2)}) collective-permute-start(bf16[3,256,128]{2,1,0:T(8,128)(2,1)S(1)} %copy-done.58), channel_id=1, source_target_pairs={{0,7},{1,6},{2,5},{3,4},{4,3},{5,2},{6,1},{7,0},{8,15},{9,14},{10,... | collective-permute-start | bytes 589832 | tf_op jit(solution)/shard_map/ppermute | solution.py:125
  313.0 32.5 %collective-permute-start.62 = (bf16[6,256,128]{2,1,0:T(8,128)(2,1)}, bf16[6,256,128]{2,1,0:T(8,128)(2,1)S(1)}, u32[]{:S(2)}, u32[]{:S(2)}) collective-permute-start(bf16[6,256,128]{2,1,0:T(8,128)(2,1)} %get-tuple-element.130), channel_id=1, source_target_pairs={{0,5},{1,4},{2,7},{3,6},{4,1},{5,0},{6,3},{7,2},{8,13},{9,12},{10,... | collective-permute-start | bytes 1179656 | tf_op jit(solution)/shard_map/ppermute | solution.py:125
  313.0 44.0 %collective-permute-start.63 = (bf16[6,256,128]{2,1,0:T(8,128)(2,1)}, bf16[6,256,128]{2,1,0:T(8,128)(2,1)S(1)}, u32[]{:S(2)}, u32[]{:S(2)}) collective-permute-start(bf16[6,256,128]{2,1,0:T(8,128)(2,1)} %get-tuple-element.131), channel_id=1, source_target_pairs={{0,6},{1,7},{2,4},{3,5},{4,2},{5,3},{6,0},{7,1},{8,14},{9,15},{10,... | collective-permute-start | bytes 1179656 | tf_op jit(solution)/shard_map/ppermute | solution.py:125
  325.8 46.3 %collective-permute-start.64 = (bf16[6,256,128]{2,1,0:T(8,128)(2,1)}, bf16[6,256,128]{2,1,0:T(8,128)(2,1)S(1)}, u32[]{:S(2)}, u32[]{:S(2)}) collective-permute-start(bf16[6,256,128]{2,1,0:T(8,128)(2,1)} %get-tuple-element.132), channel_id=1, source_target_pairs={{0,7},{1,6},{2,5},{3,4},{4,3},{5,2},{6,1},{7,0},{8,15},{9,14},{10,... | collective-permute-start | bytes 1179656 | tf_op jit(solution)/shard_map/ppermute | solution.py:125
  329.2 42.9 %collective-permute-start.51 = (bf16[6,256,128]{2,1,0:T(8,128)(2,1)}, bf16[6,256,128]{2,1,0:T(8,128)(2,1)S(1)}, u32[]{:S(2)}, u32[]{:S(2)}) collective-permute-start(bf16[6,256,128]{2,1,0:T(8,128)(2,1)} %get-tuple-element.118), channel_id=1, source_target_pairs={{0,1},{1,0},{2,3},{3,2},{4,5},{5,4},{6,7},{7,6},{8,9},{9,8},{10,11... | collective-permute-start | bytes 1179656 | tf_op jit(solution)/shard_map/ppermute | solution.py:125
  329.2 60.2 %collective-permute-start.52 = (bf16[6,256,128]{2,1,0:T(8,128)(2,1)}, bf16[6,256,128]{2,1,0:T(8,128)(2,1)}, u32[]{:S(2)}, u32[]{:S(2)}) collective-permute-start(bf16[6,256,128]{2,1,0:T(8,128)(2,1)} %get-tuple-element.119), channel_id=1, source_target_pairs={{0,2},{1,3},{2,0},{3,1},{4,6},{5,7},{6,4},{7,5},{8,10},{9,11},{10,... | collective-permute-start | bytes 1179656 | tf_op jit(solution)/shard_map/ppermute | solution.py:125
  345.5 47.3 %collective-permute-start.53 = (bf16[6,256,128]{2,1,0:T(8,128)(2,1)}, bf16[6,256,128]{2,1,0:T(8,128)(2,1)}, u32[]{:S(2)}, u32[]{:S(2)}) collective-permute-start(bf16[6,256,128]{2,1,0:T(8,128)(2,1)} %get-tuple-element.120), channel_id=1, source_target_pairs={{0,3},{1,2},{2,1},{3,0},{4,7},{5,6},{6,5},{7,4},{8,11},{9,10},{10,... | collective-permute-start | bytes 1179656 | tf_op jit(solution)/shard_map/ppermute | solution.py:125
  357.0 49.6 %collective-permute-start.54 = (bf16[6,256,128]{2,1,0:T(8,128)(2,1)}, bf16[6,256,128]{2,1,0:T(8,128)(2,1)}, u32[]{:S(2)}, u32[]{:S(2)}) collective-permute-start(bf16[6,256,128]{2,1,0:T(8,128)(2,1)} %get-tuple-element.121), channel_id=1, source_target_pairs={{0,4},{1,5},{2,6},{3,7},{4,0},{5,1},{6,2},{7,3},{8,12},{9,13},{10,... | collective-permute-start | bytes 1179656 | tf_op jit(solution)/shard_map/ppermute | solution.py:125
  372.1 44.8 %collective-permute-start.55 = (bf16[6,256,128]{2,1,0:T(8,128)(2,1)}, bf16[6,256,128]{2,1,0:T(8,128)(2,1)}, u32[]{:S(2)}, u32[]{:S(2)}) collective-permute-start(bf16[6,256,128]{2,1,0:T(8,128)(2,1)} %get-tuple-element.122), channel_id=1, source_target_pairs={{0,5},{1,4},{2,7},{3,6},{4,1},{5,0},{6,3},{7,2},{8,13},{9,12},{10,... | collective-permute-start | bytes 1179656 | tf_op jit(solution)/shard_map/ppermute | solution.py:125
  372.1 58.2 %collective-permute-start.56 = (bf16[6,256,128]{2,1,0:T(8,128)(2,1)}, bf16[6,256,128]{2,1,0:T(8,128)(2,1)}, u32[]{:S(2)}, u32[]{:S(2)}) collective-permute-start(bf16[6,256,128]{2,1,0:T(8,128)(2,1)} %get-tuple-element.123), channel_id=1, source_target_pairs={{0,6},{1,7},{2,4},{3,5},{4,2},{5,3},{6,0},{7,1},{8,14},{9,15},{10,... | collective-permute-start | bytes 1179656 | tf_op jit(solution)/shard_map/ppermute | solution.py:125
  389.5 49.9 %collective-permute-start.57 = (bf16[6,256,128]{2,1,0:T(8,128)(2,1)}, bf16[6,256,128]{2,1,0:T(8,128)(2,1)}, u32[]{:S(2)}, u32[]{:S(2)}) collective-permute-start(bf16[6,256,128]{2,1,0:T(8,128)(2,1)} %get-tuple-element.124), channel_id=1, source_target_pairs={{0,7},{1,6},{2,5},{3,4},{4,3},{5,2},{6,1},{7,0},{8,15},{9,14},{10,... | collective-permute-start | bytes 1179656 | tf_op jit(solution)/shard_map/ppermute | solution.py:125
  392.8 71.8 %collective-permute-start.39 = (bf16[1,256,128]{2,1,0:T(8,128)(2,1)}, bf16[1,256,128]{2,1,0:T(8,128)(2,1)S(1)}, u32[]{:S(2)}, u32[]{:S(2)}) collective-permute-start(bf16[1,256,128]{2,1,0:T(8,128)(2,1)} %get-tuple-element.104), channel_id=1, source_target_pairs={{0,3},{1,2},{2,1},{3,0},{4,7},{5,6},{6,5},{7,4},{8,11},{9,10},{10,... | collective-permute-start | bytes 196616 | tf_op jit(solution)/shard_map/ppermute | solution.py:125
  406.6 58.0 %collective-permute-start.40 = (bf16[1,256,128]{2,1,0:T(8,128)(2,1)}, bf16[1,256,128]{2,1,0:T(8,128)(2,1)}, u32[]{:S(2)}, u32[]{:S(2)}) collective-permute-start(bf16[1,256,128]{2,1,0:T(8,128)(2,1)} %get-tuple-element.105), channel_id=1, source_target_pairs={{0,4},{1,5},{2,6},{3,7},{4,0},{5,1},{6,2},{7,3},{8,12},{9,13},{10,... | collective-permute-start | bytes 196616 | tf_op jit(solution)/shard_map/ppermute | solution.py:125
  417.0 47.6 %collective-permute-start.41 = (bf16[1,256,128]{2,1,0:T(8,128)(2,1)}, bf16[1,256,128]{2,1,0:T(8,128)(2,1)}, u32[]{:S(2)}, u32[]{:S(2)}) collective-permute-start(bf16[1,256,128]{2,1,0:T(8,128)(2,1)} %get-tuple-element.106), channel_id=1, source_target_pairs={{0,5},{1,4},{2,7},{3,6},{4,1},{5,0},{6,3},{7,2},{8,13},{9,12},{10,... | collective-permute-start | bytes 196616 | tf_op jit(solution)/shard_map/ppermute | solution.py:125
  430.3 34.3 %collective-permute-start.42 = (bf16[1,256,128]{2,1,0:T(8,128)(2,1)}, bf16[1,256,128]{2,1,0:T(8,128)(2,1)}, u32[]{:S(2)}, u32[]{:S(2)}) collective-permute-start(bf16[1,256,128]{2,1,0:T(8,128)(2,1)} %get-tuple-element.107), channel_id=1, source_target_pairs={{0,6},{1,7},{2,4},{3,5},{4,2},{5,3},{6,0},{7,1},{8,14},{9,15},{10,... | collective-permute-start | bytes 196616 | tf_op jit(solution)/shard_map/ppermute | solution.py:125
  439.4 25.2 %collective-permute-start.43 = (bf16[1,256,128]{2,1,0:T(8,128)(2,1)}, bf16[1,256,128]{2,1,0:T(8,128)(2,1)}, u32[]{:S(2)}, u32[]{:S(2)}) collective-permute-start(bf16[1,256,128]{2,1,0:T(8,128)(2,1)} %get-tuple-element.108), channel_id=1, source_target_pairs={{0,7},{1,6},{2,5},{3,4},{4,3},{5,2},{6,1},{7,0},{8,15},{9,14},{10,... | collective-permute-start | bytes 196616 | tf_op jit(solution)/shard_map/ppermute | solution.py:125
  (65 other events, 1989.8 us)

commit v2 on v1

--- a/solution.py
+++ b/solution.py
@@ -11,8 +11,11 @@
 GATE_GROUPS = ((4, 4), (4, 4))
 UP_GROUPS = ((6, 6, 3, 1),)
 
+HALVED = 1
+
 SMEM = pl.BlockSpec(memory_space=pltpu.SMEM)
 ANY = pl.BlockSpec(memory_space=pl.ANY)
+SUBLANES = 8
 
 
 def spans(groups, experts):
@@ -34,18 +37,24 @@
     return next(n for n in range(most, 0, -1) if all(count % n == 0 for count in counts))
 
 
-def sums_body(first, step, mix_ref, w_ref, avg_ref, *refs):
-    out_ref = refs[-1]
+def sum_of(mix, w_ref, avg_ref, i):
+    held = None
+    for r in range(0, w_ref.shape[1], SUBLANES):
+        cut = slice(r, r + SUBLANES)
+        size = jnp.abs(mix * w_ref[i, cut, :] + (1.0 - mix) * avg_ref[i, cut, :])
+        held = size if held is None else held + size
+    return jnp.sum(held, axis=0, keepdims=True)
+
+
+def sums_body(first, step, mix_ref, w_ref, avg_ref, out_ref):
     for i in range(step):
         at = pl.program_id(0) * step + i
-        mix = mix_ref[first + at]
-        fresh = mix * w_ref[i] + (1.0 - mix) * avg_ref[i]
-        out_ref[pl.ds(at, 1), :] = jnp.sum(jnp.abs(fresh), axis=0, keepdims=True)
+        out_ref[pl.ds(at, 1), :] = sum_of(mix_ref[first + at], w_ref, avg_ref, i)
 
 
 def sums(mix, w, avg, first, count):
     _, rows, cols = w.shape
-    step = step_of(4 if first else 2, count, first)
+    step = step_of(4, count, first)
     block = pl.BlockSpec((step, rows, cols), lambda e: (first // step + e, 0, 0))
     return pl.pallas_call(
         functools.partial(sums_body, first, step),
@@ -57,38 +66,52 @@
     )(mix, w, avg)
 
 
-def pack_body(first, skip, ways, me_ref, mix_ref, w_ref, avg_ref, *refs):
-    addends, out_refs, held_ref = refs[: -1 - ways], refs[-1 - ways : -1], refs[-1]
-    me = me_ref[0]
+def pack_body(first, skip, ways, pieces, me_ref, mix_ref, w_ref, avg_ref, *refs):
+    addends, out_refs, held_ref = refs[: -1 - pieces], refs[-1 - pieces : -1], refs[-1]
+    low = me_ref[0] & (pieces - 1)
     step, rows, cols = w_ref.shape
-    width = cols // ways
+    width = cols // pieces
     for i in range(step):
         at = pl.program_id(0) * step + i
         mix = mix_ref[first + at]
         row = pl.ds(skip + at, 1)
         total = sum(ref[row, :] for ref in addends)
         inverse = 1.0 / (total * (1.0 / (ways * rows)))
-        for j in range(ways):
+        for j in range(pieces):
             cut = slice(j * width, (j + 1) * width)
             fresh = mix * w_ref[i, :, cut] + (1.0 - mix) * avg_ref[i, :, cut]
-            held_ref[me ^ j] = (fresh * inverse[:, cut]).astype(jnp.bfloat16)
-        for k in range(ways):
+            held_ref[low ^ j] = (fresh * inverse[:, cut]).astype(jnp.bfloat16)
+        for k in range(pieces):
             out_refs[k][i] = held_ref[k]
 
 
-def pack(me, mix, w, avg, addends, first, count, skip, ways):
+def pack(me, mix, w, avg, addends, first, count, skip, ways, part=None):
     _, rows, cols = w.shape
     step = step_of(2, count, first)
-    block = pl.BlockSpec((step, rows, cols), lambda e: (first // step + e, 0, 0))
+    pieces = ways if part is None else ways // 2
+
+    def side(me_ref):
+        if part is None:
+            return 0
+        return (me_ref[0] >> (pieces.bit_length() - 1)) ^ part
+
+    block = pl.BlockSpec(
+        (step, rows, cols * pieces // ways), lambda e, me_ref: (first // step + e, 0, side(me_ref))
+    )
+    sums_block = pl.BlockSpec(
+        (addends[0].shape[0], cols * pieces // ways), lambda e, me_ref: (0, side(me_ref))
+    )
     piece = (rows, cols // ways)
     return pl.pallas_call(
-        functools.partial(pack_body, first, skip, ways),
-        grid=(count // step,),
-        in_specs=[SMEM, SMEM, block, block]
-        + [pl.BlockSpec(addends[0].shape, lambda e: (0, 0))] * len(addends),
-        out_specs=[pl.BlockSpec((step,) + piece, lambda e: (e, 0, 0))] * ways,
-        out_shape=[jax.ShapeDtypeStruct((count,) + piece, jnp.bfloat16)] * ways,
-        scratch_shapes=[pltpu.VMEM((ways,) + piece, jnp.bfloat16)],
+        functools.partial(pack_body, first, skip, ways, pieces),
+        grid_spec=pltpu.PrefetchScalarGridSpec(
+            num_scalar_prefetch=1,
+            grid=(count // step,),
+            in_specs=[SMEM, block, block] + [sums_block] * len(addends),
+            out_specs=[pl.BlockSpec((step,) + piece, lambda e, me_ref: (e, 0, 0))] * pieces,
+            scratch_shapes=[pltpu.VMEM((pieces,) + piece, jnp.bfloat16)],
+        ),
+        out_shape=[jax.ShapeDtypeStruct((count,) + piece, jnp.bfloat16)] * pieces,
         name="pack",
     )(me, mix, w, avg, *addends)
 
@@ -126,7 +149,7 @@
 
 
 def crossings(ways):
-    return list(reversed(range(1, ways)))
+    return list(reversed(range(ways // 2, ways))) + list(range(1, ways // 2))
 
 
 def doublings(ways):
@@ -196,13 +219,18 @@
         whole, own = None, []
         for chunks in spans(shares, experts):
             start = chunks[0][0]
-            total = sums(mix_share, w, avg, start, sum(n for _, n in chunks))
+            members = sum(n for _, n in chunks)
+            total = sums(mix_share, w, avg, start, members)
             for k in doublings(ways):
                 addends = [total, swap(total, k, "zero", ways)]
                 total = addends[0] + addends[1]
             own.append(lax.dynamic_slice_in_dim(total, index * width, width, axis=1))
             for first, count in chunks:
-                sent = pack(me, mix_share, w, avg, addends, first, count, first - start, ways)
+                sent = []
+                for part in (0, 1) if g < HALVED and first == start else (None,):
+                    sent += pack(
+                        me, mix_share, w, avg, addends, first, count, first - start, ways, part
+                    )
                 received = list(sent)
                 for k in crossings(ways):
                     received[k] = swap(sent[k], k, "zero", ways)

time: 468 us -> 463 us (0.989)
  the two profiles are of different devices: /device:TPU:8 before, /device:TPU:16 now
where the time goes in v2:
time: 463 us; the launch traced here: 462 us
  waiting for transfers between devices  242 us (52%)
  starting transfers between devices  106 us (23%)
  Pallas kernels  99.9 us (22%)
  other arithmetic  7.08 us (2%)
  local copies, waits for them, and re-layouts  5.42 us (1%)
    ppermute x70, waiting for transfers between devices, swap(): return lax.ppermute(value, axis, [(d, d ^ k) for d in range(ways)])  242 us
    ppermute x70, starting transfers between devices, swap(): return lax.ppermute(value, axis, [(d, d ^ k) for d in range(ways)])  106 us
    pallas_call x9, Pallas kernels, pack(): pl.pallas_call(functools.partial(pack_body, first, skip, ways, pieces), g...  45.9 us
    pallas_call x3, Pallas kernels, sums(): pl.pallas_call(functools.partial(sums_body, first, step), grid=(count //...  26.6 us
    pallas_call x8, Pallas kernels, unpack(): pl.pallas_call(functools.partial(unpack_body, ways), grid=(count // step,...  22.9 us
  transfers between devices with their start and end apart: 70, of which 26 were waited for; matrix products, arithmetic and copies ran while one was open for 1% of the time, Pallas kernels for 21%

profile of v2, /device:TPU:16, one launch (start us, length us, event | category | flops | bytes accessed | tf_op | source)
XLA Modules:
  0.0 462.1 jit_solution(16442069295383198111)
XLA Ops:
  2.0 4.8 %collective-permute-done.65 = bf16[1,16,256]{2,1,0:T(8,128)(2,1)S(1)} collective-permute-done((bf16[1,16,256]{2,1,0:T(8,128)(2,1)}, bf16[1,16,256]{2,1,0:T(8,128)(2,1)S(1)}, u32[]{:S(2)}, u32[]{:S(2)}) %collective-permute-start.65) | collective-permute-done | bytes 8224 | tf_op jit(solution)/shard_map/ppermute | solution.py:148
  9.0 7.2 %sums.4 = f32[8,1024]{1,0:T(8,128)} custom-call(f32[16]{0:T(128)} %mix_ref.23, f32[16,256,1024]{2,1,0:T(8,128)} %w_ref.18, f32[16,256,1024]{2,1,0:T(8,128)} %avg_ref.18), custom_call_target="tpu_custom_call" | custom-call | tf_op jit(solution)/shard_map/sums/pallas_call | solution.py:59
  18.3 12.2 %sums.5 = f32[16,1024]{1,0:T(8,128)} custom-call(f32[16]{0:T(128)} %mix_ref.23, f32[16,256,1024]{2,1,0:T(8,128)} %w_ref.23, f32[16,256,1024]{2,1,0:T(8,128)} %avg_ref.23), custom_call_target="tpu_custom_call" | custom-call | tf_op jit(solution)/shard_map/sums/pallas_call | solution.py:59
  36.2 7.2 %sums.3 = f32[8,1024]{1,0:T(8,128)} custom-call(f32[16]{0:T(128)} %mix_ref.23, f32[16,256,1024]{2,1,0:T(8,128)} %w_ref.18, f32[16,256,1024]{2,1,0:T(8,128)} %avg_ref.18), custom_call_target="tpu_custom_call" | custom-call | tf_op jit(solution)/shard_map/sums/pallas_call | solution.py:59
  44.3 3.2 collective-permute-done
  51.0 3.4 pack.12
  58.5 7.5 %collective-permute-done.36.refs_1_ = f32[16,1024]{1,0:T(8,128)S(1)} collective-permute-done((f32[16,1024]{1,0:T(8,128)S(1)}, f32[16,1024]{1,0:T(8,128)S(1)}, u32[]{:S(2)}, u32[]{:S(2)}) %collective-permute-start.36) | collective-permute-done | bytes 65568 | tf_op jit(solution)/shard_map/ppermute | solution.py:148
  66.5 2.7 pack.14
  73.4 3.4 pack.13
  76.8 2.5 collective-permute-start.30
  79.3 5.2 %pack.11 = (bf16[4,256,128]{2,1,0:T(8,128)(2,1)}, bf16[4,256,128]{2,1,0:T(8,128)(2,1)}, bf16[4,256,128]{2,1,0:T(8,128)(2,1)}, bf16[4,256,128]{2,1,0:T(8,128)(2,1...) custom-call(s32[1]{0:T(128)} %bitcast.me_ref, ...), custom_call_target="tpu_custom_call" | custom-call | tf_op jit(solution)/shard_map/pack/pallas_call | solution.py:105
  89.2 16.4 %collective-permute-done.30.refs_4_ = bf16[4,256,128]{2,1,0:T(8,128)(2,1)S(1)} collective-permute-done((bf16[4,256,128]{2,1,0:T(8,128)(2,1)}, bf16[4,256,128]{2,1,0:T(8,128)(2,1)S(1)}, u32[]{:S(2)}, u32[]{:S(2)}) %collective-permute-start.30) | collective-permute-done | bytes 262176 | tf_op jit(solution)/shard_map/ppermute | solution.py:148
  106.9 4.2 collective-permute-done.31.refs_5_
  111.8 2.3 collective-permute-start.22
  114.2 3.7 collective-permute-done.32.refs_6_
  117.9 19.3 %collective-permute-done.33.refs_7_ = bf16[4,256,128]{2,1,0:T(8,128)(2,1)S(1)} collective-permute-done((bf16[4,256,128]{2,1,0:T(8,128)(2,1)S(1)}, bf16[4,256,128]{2,1,0:T(8,128)(2,1)S(1)}, u32[]{:S(2)}, u32[]{:S(2)}) %collective-permute-start.33) | collective-permute-done | bytes 262176 | tf_op jit(solution)/shard_map/ppermute | solution.py:148
  140.6 5.3 %pack.10 = (bf16[4,256,128]{2,1,0:T(8,128)(2,1)}, bf16[4,256,128]{2,1,0:T(8,128)(2,1)}, bf16[4,256,128]{2,1,0:T(8,128)(2,1)}, bf16[4,256,128]{2,1,0:T(8,128)(2,1...) custom-call(s32[1]{0:T(128)} %bitcast.me_ref, ...), custom_call_target="tpu_custom_call" | custom-call | tf_op jit(solution)/shard_map/pack/pallas_call | solution.py:105
  146.8 5.8 %collective-permute-start.11 = (bf16[4,256,128]{2,1,0:T(8,128)(2,1)}, bf16[4,256,128]{2,1,0:T(8,128)(2,1)S(1)}, u32[]{:S(2)}, u32[]{:S(2)}) collective-permute-start(bf16[4,256,128]{2,1,0:T(8,128)(2,1)} %get-tuple-element.79), channel_id=1, source_target_pairs={{0,2},{1,3},{2,0},{3,1},{4,6},{5,7},{6,4},{7,5},{8,10},{9,11},{10,... | collective-permute-start | bytes 786440 | tf_op jit(solution)/shard_map/ppermute | solution.py:148
  152.7 3.5 collective-permute-done.24.refs_5_
  156.2 2.2 collective-permute-start.12
  158.5 4.6 %collective-permute-done.25.refs_6_ = bf16[4,256,128]{2,1,0:T(8,128)(2,1)S(1)} collective-permute-done((bf16[4,256,128]{2,1,0:T(8,128)(2,1)}, bf16[4,256,128]{2,1,0:T(8,128)(2,1)S(1)}, u32[]{:S(2)}, u32[]{:S(2)}) %collective-permute-start.25) | collective-permute-done | bytes 262176 | tf_op jit(solution)/shard_map/ppermute | solution.py:148
  163.1 13.4 %collective-permute-done.26.refs_7_ = bf16[4,256,128]{2,1,0:T(8,128)(2,1)S(1)} collective-permute-done((bf16[4,256,128]{2,1,0:T(8,128)(2,1)}, bf16[4,256,128]{2,1,0:T(8,128)(2,1)S(1)}, u32[]{:S(2)}, u32[]{:S(2)}) %collective-permute-start.26) | collective-permute-done | bytes 262176 | tf_op jit(solution)/shard_map/ppermute | solution.py:148
  176.5 5.3 %pack.9 = (bf16[4,256,128]{2,1,0:T(8,128)(2,1)}, bf16[4,256,128]{2,1,0:T(8,128)(2,1)}, bf16[4,256,128]{2,1,0:T(8,128)(2,1)}, bf16[4,256,128]{2,1,0:T(8,128)(2,1)...) custom-call(s32[1]{0:T(128)} %bitcast.me_ref, ...), custom_call_target="tpu_custom_call" | custom-call | tf_op jit(solution)/shard_map/pack/pallas_call | solution.py:105
  181.9 2.0 collective-permute-start.15
  184.0 3.6 collective-permute-start.16
  189.8 4.3 collective-permute-start.4
  194.1 7.1 %collective-permute-done.14.refs_5_ = bf16[4,256,128]{2,1,0:T(8,128)(2,1)S(1)} collective-permute-done((bf16[4,256,128]{2,1,0:T(8,128)(2,1)}, bf16[4,256,128]{2,1,0:T(8,128)(2,1)S(1)}, u32[]{:S(2)}, u32[]{:S(2)}) %collective-permute-start.14) | collective-permute-done | bytes 262176 | tf_op jit(solution)/shard_map/ppermute | solution.py:148
  201.2 2.2 collective-permute-start.5
  203.5 4.7 %collective-permute-done.15.refs_6_ = bf16[4,256,128]{2,1,0:T(8,128)(2,1)S(1)} collective-permute-done((bf16[4,256,128]{2,1,0:T(8,128)(2,1)}, bf16[4,256,128]{2,1,0:T(8,128)(2,1)S(1)}, u32[]{:S(2)}, u32[]{:S(2)}) %collective-permute-start.15) | collective-permute-done | bytes 262176 | tf_op jit(solution)/shard_map/ppermute | solution.py:148
  208.1 19.0 %collective-permute-done.16.refs_7_ = bf16[4,256,128]{2,1,0:T(8,128)(2,1)S(1)} collective-permute-done((bf16[4,256,128]{2,1,0:T(8,128)(2,1)S(1)}, bf16[4,256,128]{2,1,0:T(8,128)(2,1)S(1)}, u32[]{:S(2)}, u32[]{:S(2)}) %collective-permute-start.16) | collective-permute-done | bytes 262176 | tf_op jit(solution)/shard_map/ppermute | solution.py:148
  227.2 2.0 collective-permute-start.8
  229.9 5.0 %pack.15 = (bf16[3,256,128]{2,1,0:T(8,128)(2,1)}, bf16[3,256,128]{2,1,0:T(8,128)(2,1)}, bf16[3,256,128]{2,1,0:T(8,128)(2,1)}, bf16[3,256,128]{2,1,0:T(8,128)(2,1...) custom-call(s32[1]{0:T(128)} %bitcast.me_ref, ...), custom_call_target="tpu_custom_call" | custom-call | tf_op jit(solution)/shard_map/pack/pallas_call | solution.py:105
  235.9 5.8 %collective-permute-start.45 = (bf16[3,256,128]{2,1,0:T(8,128)(2,1)}, bf16[3,256,128]{2,1,0:T(8,128)(2,1)S(1)}, u32[]{:S(2)}, u32[]{:S(2)}) collective-permute-start(bf16[3,256,128]{2,1,0:T(8,128)(2,1)} %get-tuple-element.111), channel_id=1, source_target_pairs={{0,2},{1,3},{2,0},{3,1},{4,6},{5,7},{6,4},{7,5},{8,10},{9,11},{10,... | collective-permute-start | bytes 589832 | tf_op jit(solution)/shard_map/ppermute | solution.py:148
  241.7 4.5 collective-permute-done.7.refs_5_
  246.2 2.2 collective-permute-start.46
  248.4 5.4 %collective-permute-done.8.refs_6_ = bf16[4,256,128]{2,1,0:T(8,128)(2,1)} collective-permute-done((bf16[4,256,128]{2,1,0:T(8,128)(2,1)}, bf16[4,256,128]{2,1,0:T(8,128)(2,1)}, u32[]{:S(2)}, u32[]{:S(2)}) %collective-permute-start.8) | collective-permute-done | bytes 262176 | tf_op jit(solution)/shard_map/ppermute | solution.py:148
  253.8 12.7 %collective-permute-done.9.refs_7_ = bf16[4,256,128]{2,1,0:T(8,128)(2,1)} collective-permute-done((bf16[4,256,128]{2,1,0:T(8,128)(2,1)}, bf16[4,256,128]{2,1,0:T(8,128)(2,1)}, u32[]{:S(2)}, u32[]{:S(2)}) %collective-permute-start.9) | collective-permute-done | bytes 262176 | tf_op jit(solution)/shard_map/ppermute | solution.py:148
  266.6 2.0 collective-permute-start.49
  268.6 7.8 %pack.17 = (bf16[6,256,128]{2,1,0:T(8,128)(2,1)}, bf16[6,256,128]{2,1,0:T(8,128)(2,1)}, bf16[6,256,128]{2,1,0:T(8,128)(2,1)}, bf16[6,256,128]{2,1,0:T(8,128)(2,1...) custom-call(s32[1]{0:T(128)} %bitcast.me_ref, ...), custom_call_target="tpu_custom_call" | custom-call | tf_op jit(solution)/shard_map/pack/pallas_call | solution.py:105
  278.6 2.5 collective-permute-start.59
  281.9 4.1 collective-permute-start.61
  286.3 7.8 %pack.16 = (bf16[6,256,128]{2,1,0:T(8,128)(2,1)}, bf16[6,256,128]{2,1,0:T(8,128)(2,1)}, bf16[6,256,128]{2,1,0:T(8,128)(2,1)}, bf16[6,256,128]{2,1,0:T(8,128)(2,1...) custom-call(s32[1]{0:T(128)} %bitcast.me_ref, ...), custom_call_target="tpu_custom_call" | custom-call | tf_op jit(solution)/shard_map/pack/pallas_call | solution.py:105
  294.2 25.9 %collective-permute-done.50.refs_7_ = bf16[3,256,128]{2,1,0:T(8,128)(2,1)S(1)} collective-permute-done((bf16[3,256,128]{2,1,0:T(8,128)(2,1)S(1)}, bf16[3,256,128]{2,1,0:T(8,128)(2,1)S(1)}, u32[]{:S(2)}, u32[]{:S(2)}) %collective-permute-start.50) | collective-permute-done | bytes 196640 | tf_op jit(solution)/shard_map/ppermute | solution.py:148
  320.1 3.7 collective-permute-start.63
  325.4 4.6 %collective-permute-start.52 = (bf16[6,256,128]{2,1,0:T(8,128)(2,1)}, bf16[6,256,128]{2,1,0:T(8,128)(2,1)}, u32[]{:S(2)}, u32[]{:S(2)}) collective-permute-start(bf16[6,256,128]{2,1,0:T(8,128)(2,1)} %get-tuple-element.119), channel_id=1, source_target_pairs={{0,2},{1,3},{2,0},{3,1},{4,6},{5,7},{6,4},{7,5},{8,10},{9,11},{10,... | collective-permute-start | bytes 1179656 | tf_op jit(solution)/shard_map/ppermute | solution.py:148
  330.0 12.4 %collective-permute-done.62.refs_5_ = bf16[6,256,128]{2,1,0:T(8,128)(2,1)S(1)} collective-permute-done((bf16[6,256,128]{2,1,0:T(8,128)(2,1)}, bf16[6,256,128]{2,1,0:T(8,128)(2,1)S(1)}, u32[]{:S(2)}, u32[]{:S(2)}) %collective-permute-start.62) | collective-permute-done | bytes 393248 | tf_op jit(solution)/shard_map/ppermute | solution.py:148
  342.4 6.5 %collective-permute-start.53 = (bf16[6,256,128]{2,1,0:T(8,128)(2,1)}, bf16[6,256,128]{2,1,0:T(8,128)(2,1)}, u32[]{:S(2)}, u32[]{:S(2)}) collective-permute-start(bf16[6,256,128]{2,1,0:T(8,128)(2,1)} %get-tuple-element.120), channel_id=1, source_target_pairs={{0,3},{1,2},{2,1},{3,0},{4,7},{5,6},{6,5},{7,4},{8,11},{9,10},{10,... | collective-permute-start | bytes 1179656 | tf_op jit(solution)/shard_map/ppermute | solution.py:148
  348.9 10.3 %collective-permute-done.63.refs_6_ = bf16[6,256,128]{2,1,0:T(8,128)(2,1)S(1)} collective-permute-done((bf16[6,256,128]{2,1,0:T(8,128)(2,1)}, bf16[6,256,128]{2,1,0:T(8,128)(2,1)S(1)}, u32[]{:S(2)}, u32[]{:S(2)}) %collective-permute-start.63) | collective-permute-done | bytes 393248 | tf_op jit(solution)/shard_map/ppermute | solution.py:148
  359.2 24.4 %collective-permute-done.64.refs_7_ = bf16[6,256,128]{2,1,0:T(8,128)(2,1)S(1)} collective-permute-done((bf16[6,256,128]{2,1,0:T(8,128)(2,1)}, bf16[6,256,128]{2,1,0:T(8,128)(2,1)S(1)}, u32[]{:S(2)}, u32[]{:S(2)}) %collective-permute-start.64) | collective-permute-done | bytes 393248 | tf_op jit(solution)/shard_map/ppermute | solution.py:148
  384.2 3.3 collective-permute-start.57
  390.8 3.3 collective-permute-start.39
  394.0 8.2 %collective-permute-done.54.refs_4_ = bf16[6,256,128]{2,1,0:T(8,128)(2,1)} collective-permute-done((bf16[6,256,128]{2,1,0:T(8,128)(2,1)}, bf16[6,256,128]{2,1,0:T(8,128)(2,1)}, u32[]{:S(2)}, u32[]{:S(2)}) %collective-permute-start.54) | collective-permute-done | bytes 393248 | tf_op jit(solution)/shard_map/ppermute | solution.py:148
  402.3 3.4 collective-permute-start.40
  405.7 7.8 %collective-permute-done.55.refs_5_ = bf16[6,256,128]{2,1,0:T(8,128)(2,1)} collective-permute-done((bf16[6,256,128]{2,1,0:T(8,128)(2,1)}, bf16[6,256,128]{2,1,0:T(8,128)(2,1)}, u32[]{:S(2)}, u32[]{:S(2)}) %collective-permute-start.55) | collective-permute-done | bytes 393248 | tf_op jit(solution)/shard_map/ppermute | solution.py:148
  413.5 4.3 collective-permute-start.41
  417.8 9.9 %collective-permute-done.56.refs_6_ = bf16[6,256,128]{2,1,0:T(8,128)(2,1)} collective-permute-done((bf16[6,256,128]{2,1,0:T(8,128)(2,1)}, bf16[6,256,128]{2,1,0:T(8,128)(2,1)}, u32[]{:S(2)}, u32[]{:S(2)}) %collective-permute-start.56) | collective-permute-done | bytes 393248 | tf_op jit(solution)/shard_map/ppermute | solution.py:148
  427.7 5.6 %collective-permute-done.57.refs_7_ = bf16[6,256,128]{2,1,0:T(8,128)(2,1)} collective-permute-done((bf16[6,256,128]{2,1,0:T(8,128)(2,1)}, bf16[6,256,128]{2,1,0:T(8,128)(2,1)}, u32[]{:S(2)}, u32[]{:S(2)}) %collective-permute-start.57) | collective-permute-done | bytes 393248 | tf_op jit(solution)/shard_map/ppermute | solution.py:148
  438.5 3.0 unpack.8.refs_8_
  441.5 3.0 unpack.9.refs_8_
  444.5 3.0 unpack.10.refs_8_
  447.4 3.0 unpack.11
  450.4 3.2 unpack.12.refs_8_
  453.6 3.2 unpack.13.refs_8_
  456.9 2.7 unpack.14.refs_8_
  (230 shorter events, 55.9 us)
Async XLA Ops:
  7.4 10.3 %collective-permute-start.66 = (bf16[2,16,256]{2,1,0:T(8,128)(2,1)S(1)}, bf16[2,16,256]{2,1,0:T(8,128)(2,1)S(1)}, u32[]{:S(2)}, u32[]{:S(2)}) collective-permute-start(bf16[2,16,256]{2,1,0:T(8,128)(2,1)S(1)} %pad_maximum_fusion.4), channel_id=1, source_target_pairs={{0,2},{1,3},{2,0},{3,1},{4,6},{5,7},{6,4},{7,5},{8,10},{9,11},{10,... | collective-permute-start | bytes 49160 | tf_op jit(solution)/shard_map/ppermute | solution.py:148
  16.2 15.9 %collective-permute-start.17 = (f32[8,1024]{1,0:T(8,128)}, f32[8,1024]{1,0:T(8,128)S(1)}, u32[]{:S(2)}, u32[]{:S(2)}) collective-permute-start(f32[8,1024]{1,0:T(8,128)} %sums.4), channel_id=1, source_target_pairs={{0,1},{1,0},{2,3},{3,2},{4,5},{5,4},{6,7},{7,6},{8,9},{9,8},{10,11... | collective-permute-start | bytes 98312 | tf_op jit(solution)/shard_map/ppermute | solution.py:148
  17.7 14.8 %collective-permute-start.67 = (bf16[4,16,256]{2,1,0:T(8,128)(2,1)S(1)}, bf16[4,16,256]{2,1,0:T(8,128)(2,1)S(1)}, u32[]{:S(2)}, u32[]{:S(2)}) collective-permute-start(bf16[4,16,256]{2,1,0:T(8,128)(2,1)S(1)} %pad_maximum_fusion.3), channel_id=1, source_target_pairs={{0,1},{1,0},{2,3},{3,2},{4,5},{5,4},{6,7},{7,6},{8,9},{9,8},{10,11... | collective-permute-start | bytes 98312 | tf_op jit(solution)/shard_map/ppermute | solution.py:148
  30.5 19.3 %collective-permute-start.34 = (f32[16,1024]{1,0:T(8,128)}, f32[16,1024]{1,0:T(8,128)S(1)}, u32[]{:S(2)}, u32[]{:S(2)}) collective-permute-start(f32[16,1024]{1,0:T(8,128)} %sums.5), channel_id=1, source_target_pairs={{0,1},{1,0},{2,3},{3,2},{4,5},{5,4},{6,7},{7,6},{8,9},{9,8},{10,11... | collective-permute-start | bytes 196616 | tf_op jit(solution)/shard_map/ppermute | solution.py:148
  32.0 11.8 %collective-permute-start.18 = (f32[8,1024]{1,0:T(8,128)S(1)}, f32[8,1024]{1,0:T(8,128)S(1)}, u32[]{:S(2)}, u32[]{:S(2)}) collective-permute-start(f32[8,1024]{1,0:T(8,128)S(1)} %add.34), channel_id=1, source_target_pairs={{0,2},{1,3},{2,0},{3,1},{4,6},{5,7},{6,4},{7,5},{8,10},{9,11},{10,... | collective-permute-start | bytes 98312 | tf_op jit(solution)/shard_map/ppermute | solution.py:148
  34.7 21.8 %collective-permute-start.68 = (bf16[1,16,2048]{2,1,0:T(8,128)(2,1)}, bf16[1,16,2048]{2,1,0:T(8,128)(2,1)S(1)}, u32[]{:S(2)}, u32[]{:S(2)}) collective-permute-start(bf16[1,16,2048]{2,1,0:T(8,128)(2,1)} %bitcast.7), channel_id=1, source_target_pairs={{0,16},{8,24},{16,0},{24,8},{1,17},{9,25},{17,1},{25,9},{2,18},{10... | collective-permute-start | bytes 196616 | tf_op jit(solution)/shard_map/ppermute | solution.py:148
  48.3 9.8 %collective-permute-start.1 = (f32[8,1024]{1,0:T(8,128)S(1)}, f32[8,1024]{1,0:T(8,128)S(1)}, u32[]{:S(2)}, u32[]{:S(2)}) collective-permute-start(f32[8,1024]{1,0:T(8,128)S(1)} %add.32), channel_id=1, source_target_pairs={{0,2},{1,3},{2,0},{3,1},{4,6},{5,7},{6,4},{7,5},{8,10},{9,11},{10,... | collective-permute-start | bytes 98312 | tf_op jit(solution)/shard_map/ppermute | solution.py:148
  49.9 8.0 %collective-permute-start.35 = (f32[16,1024]{1,0:T(8,128)S(1)}, f32[16,1024]{1,0:T(8,128)S(1)}, u32[]{:S(2)}, u32[]{:S(2)}) collective-permute-start(f32[16,1024]{1,0:T(8,128)S(1)} %add.36), channel_id=1, source_target_pairs={{0,2},{1,3},{2,0},{3,1},{4,6},{5,7},{6,4},{7,5},{8,10},{9,11},{10,... | collective-permute-start | bytes 196616 | tf_op jit(solution)/shard_map/ppermute | solution.py:148
  54.4 31.2 %collective-permute-start.27 = (bf16[4,256,128]{2,1,0:T(8,128)(2,1)}, bf16[4,256,128]{2,1,0:T(8,128)(2,1)S(1)}, u32[]{:S(2)}, u32[]{:S(2)}) collective-permute-start(bf16[4,256,128]{2,1,0:T(8,128)(2,1)} %get-tuple-element.94), channel_id=1, source_target_pairs={{0,1},{1,0},{2,3},{3,2},{4,5},{5,4},{6,7},{7,6},{8,9},{9,8},{10,11... | collective-permute-start | bytes 786440 | tf_op jit(solution)/shard_map/ppermute | solution.py:148
  54.9 32.3 %collective-permute-start.28 = (bf16[4,256,128]{2,1,0:T(8,128)(2,1)}, bf16[4,256,128]{2,1,0:T(8,128)(2,1)S(1)}, u32[]{:S(2)}, u32[]{:S(2)}) collective-permute-start(bf16[4,256,128]{2,1,0:T(8,128)(2,1)} %get-tuple-element.95), channel_id=1, source_target_pairs={{0,2},{1,3},{2,0},{3,1},{4,6},{5,7},{6,4},{7,5},{8,10},{9,11},{10,... | collective-permute-start | bytes 786440 | tf_op jit(solution)/shard_map/ppermute | solution.py:148
  56.5 32.3 %collective-permute-start.29 = (bf16[4,256,128]{2,1,0:T(8,128)(2,1)}, bf16[4,256,128]{2,1,0:T(8,128)(2,1)S(1)}, u32[]{:S(2)}, u32[]{:S(2)}) collective-permute-start(bf16[4,256,128]{2,1,0:T(8,128)(2,1)} %get-tuple-element.96), channel_id=1, source_target_pairs={{0,3},{1,2},{2,1},{3,0},{4,7},{5,6},{6,5},{7,4},{8,11},{9,10},{10,... | collective-permute-start | bytes 786440 | tf_op jit(solution)/shard_map/ppermute | solution.py:148
  57.9 14.0 %collective-permute-start.69 = (bf16[2,16,2048]{2,1,0:T(8,128)(2,1)S(1)}, bf16[2,16,2048]{2,1,0:T(8,128)(2,1)S(1)}, u32[]{:S(2)}, u32[]{:S(2)}) collective-permute-start(bf16[2,16,2048]{2,1,0:T(8,128)(2,1)S(1)} %pad_maximum_fusion.1), channel_id=1, source_target_pairs={{0,8},{8,0},{16,24},{24,16},{1,9},{9,1},{17,25},{25,17},{2,10},{10... | collective-permute-start | bytes 393224 | tf_op jit(solution)/shard_map/ppermute | solution.py:148
  71.9 12.6 %collective-permute-start.38 = (bf16[1,256,128]{2,1,0:T(8,128)(2,1)}, bf16[1,256,128]{2,1,0:T(8,128)(2,1)S(1)}, u32[]{:S(2)}, u32[]{:S(2)}) collective-permute-start(bf16[1,256,128]{2,1,0:T(8,128)(2,1)} %get-tuple-element.103), channel_id=1, source_target_pairs={{0,2},{1,3},{2,0},{3,1},{4,6},{5,7},{6,4},{7,5},{8,10},{9,11},{10,... | collective-permute-start | bytes 196616 | tf_op jit(solution)/shard_map/ppermute | solution.py:148
  76.8 28.8 %collective-permute-start.30 = (bf16[4,256,128]{2,1,0:T(8,128)(2,1)}, bf16[4,256,128]{2,1,0:T(8,128)(2,1)S(1)}, u32[]{:S(2)}, u32[]{:S(2)}) collective-permute-start(bf16[4,256,128]{2,1,0:T(8,128)(2,1)} %get-tuple-element.97), channel_id=1, source_target_pairs={{0,4},{1,5},{2,6},{3,7},{4,0},{5,1},{6,2},{7,3},{8,12},{9,13},{10,... | collective-permute-start | bytes 786440 | tf_op jit(solution)/shard_map/ppermute | solution.py:148
  85.2 25.9 %collective-permute-start.31 = (bf16[4,256,128]{2,1,0:T(8,128)(2,1)S(1)}, bf16[4,256,128]{2,1,0:T(8,128)(2,1)S(1)}, u32[]{:S(2)}, u32[]{:S(2)}) collective-permute-start(bf16[4,256,128]{2,1,0:T(8,128)(2,1)S(1)} %copy-done.56), channel_id=1, source_target_pairs={{0,5},{1,4},{2,7},{3,6},{4,1},{5,0},{6,3},{7,2},{8,13},{9,12},{10,... | collective-permute-start | bytes 786440 | tf_op jit(solution)/shard_map/ppermute | solution.py:148
  85.5 32.4 %collective-permute-start.32 = (bf16[4,256,128]{2,1,0:T(8,128)(2,1)S(1)}, bf16[4,256,128]{2,1,0:T(8,128)(2,1)S(1)}, u32[]{:S(2)}, u32[]{:S(2)}) collective-permute-start(bf16[4,256,128]{2,1,0:T(8,128)(2,1)S(1)} %copy-done.55), channel_id=1, source_target_pairs={{0,6},{1,7},{2,4},{3,5},{4,2},{5,3},{6,0},{7,1},{8,14},{9,15},{10,... | collective-permute-start | bytes 786440 | tf_op jit(solution)/shard_map/ppermute | solution.py:148
  87.2 50.0 %collective-permute-start.33 = (bf16[4,256,128]{2,1,0:T(8,128)(2,1)S(1)}, bf16[4,256,128]{2,1,0:T(8,128)(2,1)S(1)}, u32[]{:S(2)}, u32[]{:S(2)}) collective-permute-start(bf16[4,256,128]{2,1,0:T(8,128)(2,1)S(1)} %copy-done.54), channel_id=1, source_target_pairs={{0,7},{1,6},{2,5},{3,4},{4,3},{5,2},{6,1},{7,0},{8,15},{9,14},{10,... | collective-permute-start | bytes 786440 | tf_op jit(solution)/shard_map/ppermute | solution.py:148
  88.8 49.2 %collective-permute-start.20 = (bf16[4,256,128]{2,1,0:T(8,128)(2,1)}, bf16[4,256,128]{2,1,0:T(8,128)(2,1)}, u32[]{:S(2)}, u32[]{:S(2)}) collective-permute-start(bf16[4,256,128]{2,1,0:T(8,128)(2,1)} %get-tuple-element.86), channel_id=1, source_target_pairs={{0,1},{1,0},{2,3},{3,2},{4,5},{5,4},{6,7},{7,6},{8,9},{9,8},{10,11... | collective-permute-start | bytes 786440 | tf_op jit(solution)/shard_map/ppermute | solution.py:148
  105.6 34.3 %collective-permute-start.21 = (bf16[4,256,128]{2,1,0:T(8,128)(2,1)}, bf16[4,256,128]{2,1,0:T(8,128)(2,1)}, u32[]{:S(2)}, u32[]{:S(2)}) collective-permute-start(bf16[4,256,128]{2,1,0:T(8,128)(2,1)} %get-tuple-element.87), channel_id=1, source_target_pairs={{0,2},{1,3},{2,0},{3,1},{4,6},{5,7},{6,4},{7,5},{8,10},{9,11},{10,... | collective-permute-start | bytes 786440 | tf_op jit(solution)/shard_map/ppermute | solution.py:148
  111.8 34.1 %collective-permute-start.22 = (bf16[4,256,128]{2,1,0:T(8,128)(2,1)}, bf16[4,256,128]{2,1,0:T(8,128)(2,1)S(1)}, u32[]{:S(2)}, u32[]{:S(2)}) collective-permute-start(bf16[4,256,128]{2,1,0:T(8,128)(2,1)} %get-tuple-element.88), channel_id=1, source_target_pairs={{0,3},{1,2},{2,1},{3,0},{4,7},{5,6},{6,5},{7,4},{8,11},{9,10},{10,... | collective-permute-start | bytes 786440 | tf_op jit(solution)/shard_map/ppermute | solution.py:148
  117.9 28.9 %collective-permute-start.23 = (bf16[4,256,128]{2,1,0:T(8,128)(2,1)}, bf16[4,256,128]{2,1,0:T(8,128)(2,1)S(1)}, u32[]{:S(2)}, u32[]{:S(2)}) collective-permute-start(bf16[4,256,128]{2,1,0:T(8,128)(2,1)} %get-tuple-element.89), channel_id=1, source_target_pairs={{0,4},{1,5},{2,6},{3,7},{4,0},{5,1},{6,2},{7,3},{8,12},{9,13},{10,... | collective-permute-start | bytes 786440 | tf_op jit(solution)/shard_map/ppermute | solution.py:148
  137.9 18.3 %collective-permute-start.24 = (bf16[4,256,128]{2,1,0:T(8,128)(2,1)}, bf16[4,256,128]{2,1,0:T(8,128)(2,1)S(1)}, u32[]{:S(2)}, u32[]{:S(2)}) collective-permute-start(bf16[4,256,128]{2,1,0:T(8,128)(2,1)} %get-tuple-element.90), channel_id=1, source_target_pairs={{0,5},{1,4},{2,7},{3,6},{4,1},{5,0},{6,3},{7,2},{8,13},{9,12},{10,... | collective-permute-start | bytes 786440 | tf_op jit(solution)/shard_map/ppermute | solution.py:148
  137.9 25.2 %collective-permute-start.25 = (bf16[4,256,128]{2,1,0:T(8,128)(2,1)}, bf16[4,256,128]{2,1,0:T(8,128)(2,1)S(1)}, u32[]{:S(2)}, u32[]{:S(2)}) collective-permute-start(bf16[4,256,128]{2,1,0:T(8,128)(2,1)} %get-tuple-element.91), channel_id=1, source_target_pairs={{0,6},{1,7},{2,4},{3,5},{4,2},{5,3},{6,0},{7,1},{8,14},{9,15},{10,... | collective-permute-start | bytes 786440 | tf_op jit(solution)/shard_map/ppermute | solution.py:148
  139.9 36.7 %collective-permute-start.26 = (bf16[4,256,128]{2,1,0:T(8,128)(2,1)}, bf16[4,256,128]{2,1,0:T(8,128)(2,1)S(1)}, u32[]{:S(2)}, u32[]{:S(2)}) collective-permute-start(bf16[4,256,128]{2,1,0:T(8,128)(2,1)} %get-tuple-element.92), channel_id=1, source_target_pairs={{0,7},{1,6},{2,5},{3,4},{4,3},{5,2},{6,1},{7,0},{8,15},{9,14},{10,... | collective-permute-start | bytes 786440 | tf_op jit(solution)/shard_map/ppermute | solution.py:148
  145.9 36.0 %collective-permute-start.10 = (bf16[4,256,128]{2,1,0:T(8,128)(2,1)}, bf16[4,256,128]{2,1,0:T(8,128)(2,1)S(1)}, u32[]{:S(2)}, u32[]{:S(2)}) collective-permute-start(bf16[4,256,128]{2,1,0:T(8,128)(2,1)} %get-tuple-element.78), channel_id=1, source_target_pairs={{0,1},{1,0},{2,3},{3,2},{4,5},{5,4},{6,7},{7,6},{8,9},{9,8},{10,11... | collective-permute-start | bytes 786440 | tf_op jit(solution)/shard_map/ppermute | solution.py:148
  146.8 37.1 %collective-permute-start.11 = (bf16[4,256,128]{2,1,0:T(8,128)(2,1)}, bf16[4,256,128]{2,1,0:T(8,128)(2,1)S(1)}, u32[]{:S(2)}, u32[]{:S(2)}) collective-permute-start(bf16[4,256,128]{2,1,0:T(8,128)(2,1)} %get-tuple-element.79), channel_id=1, source_target_pairs={{0,2},{1,3},{2,0},{3,1},{4,6},{5,7},{6,4},{7,5},{8,10},{9,11},{10,... | collective-permute-start | bytes 786440 | tf_op jit(solution)/shard_map/ppermute | solution.py:148
  156.2 31.3 %collective-permute-start.12 = (bf16[4,256,128]{2,1,0:T(8,128)(2,1)}, bf16[4,256,128]{2,1,0:T(8,128)(2,1)S(1)}, u32[]{:S(2)}, u32[]{:S(2)}) collective-permute-start(bf16[4,256,128]{2,1,0:T(8,128)(2,1)} %get-tuple-element.80), channel_id=1, source_target_pairs={{0,3},{1,2},{2,1},{3,0},{4,7},{5,6},{6,5},{7,4},{8,11},{9,10},{10,... | collective-permute-start | bytes 786440 | tf_op jit(solution)/shard_map/ppermute | solution.py:148
  163.1 26.7 %collective-permute-start.13 = (bf16[4,256,128]{2,1,0:T(8,128)(2,1)}, bf16[4,256,128]{2,1,0:T(8,128)(2,1)S(1)}, u32[]{:S(2)}, u32[]{:S(2)}) collective-permute-start(bf16[4,256,128]{2,1,0:T(8,128)(2,1)} %get-tuple-element.81), channel_id=1, source_target_pairs={{0,4},{1,5},{2,6},{3,7},{4,0},{5,1},{6,2},{7,3},{8,12},{9,13},{10,... | collective-permute-start | bytes 786440 | tf_op jit(solution)/shard_map/ppermute | solution.py:148
  176.5 24.7 %collective-permute-start.14 = (bf16[4,256,128]{2,1,0:T(8,128)(2,1)}, bf16[4,256,128]{2,1,0:T(8,128)(2,1)S(1)}, u32[]{:S(2)}, u32[]{:S(2)}) collective-permute-start(bf16[4,256,128]{2,1,0:T(8,128)(2,1)} %get-tuple-element.82), channel_id=1, source_target_pairs={{0,5},{1,4},{2,7},{3,6},{4,1},{5,0},{6,3},{7,2},{8,13},{9,12},{10,... | collective-permute-start | bytes 786440 | tf_op jit(solution)/shard_map/ppermute | solution.py:148
  181.9 26.2 %collective-permute-start.15 = (bf16[4,256,128]{2,1,0:T(8,128)(2,1)}, bf16[4,256,128]{2,1,0:T(8,128)(2,1)S(1)}, u32[]{:S(2)}, u32[]{:S(2)}) collective-permute-start(bf16[4,256,128]{2,1,0:T(8,128)(2,1)} %get-tuple-element.83), channel_id=1, source_target_pairs={{0,6},{1,7},{2,4},{3,5},{4,2},{5,3},{6,0},{7,1},{8,14},{9,15},{10,... | collective-permute-start | bytes 786440 | tf_op jit(solution)/shard_map/ppermute | solution.py:148
  184.0 43.2 %collective-permute-start.16 = (bf16[4,256,128]{2,1,0:T(8,128)(2,1)S(1)}, bf16[4,256,128]{2,1,0:T(8,128)(2,1)S(1)}, u32[]{:S(2)}, u32[]{:S(2)}) collective-permute-start(bf16[4,256,128]{2,1,0:T(8,128)(2,1)S(1)} %copy-done.53), channel_id=1, source_target_pairs={{0,7},{1,6},{2,5},{3,4},{4,3},{5,2},{6,1},{7,0},{8,15},{9,14},{10,... | collective-permute-start | bytes 786440 | tf_op jit(solution)/shard_map/ppermute | solution.py:148
  187.5 39.6 %collective-permute-start.3 = (bf16[4,256,128]{2,1,0:T(8,128)(2,1)}, bf16[4,256,128]{2,1,0:T(8,128)(2,1)S(1)}, u32[]{:S(2)}, u32[]{:S(2)}) collective-permute-start(bf16[4,256,128]{2,1,0:T(8,128)(2,1)} %get-tuple-element.70), channel_id=1, source_target_pairs={{0,1},{1,0},{2,3},{3,2},{4,5},{5,4},{6,7},{7,6},{8,9},{9,8},{10,11... | collective-permute-start | bytes 786440 | tf_op jit(solution)/shard_map/ppermute | solution.py:148
  189.8 39.3 %collective-permute-start.4 = (bf16[4,256,128]{2,1,0:T(8,128)(2,1)}, bf16[4,256,128]{2,1,0:T(8,128)(2,1)S(1)}, u32[]{:S(2)}, u32[]{:S(2)}) collective-permute-start(bf16[4,256,128]{2,1,0:T(8,128)(2,1)} %get-tuple-element.71), channel_id=1, source_target_pairs={{0,2},{1,3},{2,0},{3,1},{4,6},{5,7},{6,4},{7,5},{8,10},{9,11},{10,... | collective-permute-start | bytes 786440 | tf_op jit(solution)/shard_map/ppermute | solution.py:148
  201.2 33.8 %collective-permute-start.5 = (bf16[4,256,128]{2,1,0:T(8,128)(2,1)}, bf16[4,256,128]{2,1,0:T(8,128)(2,1)S(1)}, u32[]{:S(2)}, u32[]{:S(2)}) collective-permute-start(bf16[4,256,128]{2,1,0:T(8,128)(2,1)} %get-tuple-element.72), channel_id=1, source_target_pairs={{0,3},{1,2},{2,1},{3,0},{4,7},{5,6},{6,5},{7,4},{8,11},{9,10},{10,... | collective-permute-start | bytes 786440 | tf_op jit(solution)/shard_map/ppermute | solution.py:148
  208.1 27.8 %collective-permute-start.6 = (bf16[4,256,128]{2,1,0:T(8,128)(2,1)}, bf16[4,256,128]{2,1,0:T(8,128)(2,1)S(1)}, u32[]{:S(2)}, u32[]{:S(2)}) collective-permute-start(bf16[4,256,128]{2,1,0:T(8,128)(2,1)} %get-tuple-element.73), channel_id=1, source_target_pairs={{0,4},{1,5},{2,6},{3,7},{4,0},{5,1},{6,2},{7,3},{8,12},{9,13},{10,... | collective-permute-start | bytes 786440 | tf_op jit(solution)/shard_map/ppermute | solution.py:148
  227.1 19.1 %collective-permute-start.7 = (bf16[4,256,128]{2,1,0:T(8,128)(2,1)}, bf16[4,256,128]{2,1,0:T(8,128)(2,1)S(1)}, u32[]{:S(2)}, u32[]{:S(2)}) collective-permute-start(bf16[4,256,128]{2,1,0:T(8,128)(2,1)} %get-tuple-element.74), channel_id=1, source_target_pairs={{0,5},{1,4},{2,7},{3,6},{4,1},{5,0},{6,3},{7,2},{8,13},{9,12},{10,... | collective-permute-start | bytes 786440 | tf_op jit(solution)/shard_map/ppermute | solution.py:148
  227.2 26.7 %collective-permute-start.8 = (bf16[4,256,128]{2,1,0:T(8,128)(2,1)}, bf16[4,256,128]{2,1,0:T(8,128)(2,1)}, u32[]{:S(2)}, u32[]{:S(2)}) collective-permute-start(bf16[4,256,128]{2,1,0:T(8,128)(2,1)} %get-tuple-element.75), channel_id=1, source_target_pairs={{0,6},{1,7},{2,4},{3,5},{4,2},{5,3},{6,0},{7,1},{8,14},{9,15},{10,... | collective-permute-start | bytes 786440 | tf_op jit(solution)/shard_map/ppermute | solution.py:148
  229.2 37.4 %collective-permute-start.9 = (bf16[4,256,128]{2,1,0:T(8,128)(2,1)}, bf16[4,256,128]{2,1,0:T(8,128)(2,1)}, u32[]{:S(2)}, u32[]{:S(2)}) collective-permute-start(bf16[4,256,128]{2,1,0:T(8,128)(2,1)} %get-tuple-element.76), channel_id=1, source_target_pairs={{0,7},{1,6},{2,5},{3,4},{4,3},{5,2},{6,1},{7,0},{8,15},{9,14},{10,... | collective-permute-start | bytes 786440 | tf_op jit(solution)/shard_map/ppermute | solution.py:148
  235.0 31.5 %collective-permute-start.44 = (bf16[3,256,128]{2,1,0:T(8,128)(2,1)}, bf16[3,256,128]{2,1,0:T(8,128)(2,1)S(1)}, u32[]{:S(2)}, u32[]{:S(2)}) collective-permute-start(bf16[3,256,128]{2,1,0:T(8,128)(2,1)} %get-tuple-element.110), channel_id=1, source_target_pairs={{0,1},{1,0},{2,3},{3,2},{4,5},{5,4},{6,7},{7,6},{8,9},{9,8},{10,11... | collective-permute-start | bytes 589832 | tf_op jit(solution)/shard_map/ppermute | solution.py:148
  235.9 40.6 %collective-permute-start.45 = (bf16[3,256,128]{2,1,0:T(8,128)(2,1)}, bf16[3,256,128]{2,1,0:T(8,128)(2,1)S(1)}, u32[]{:S(2)}, u32[]{:S(2)}) collective-permute-start(bf16[3,256,128]{2,1,0:T(8,128)(2,1)} %get-tuple-element.111), channel_id=1, source_target_pairs={{0,2},{1,3},{2,0},{3,1},{4,6},{5,7},{6,4},{7,5},{8,10},{9,11},{10,... | collective-permute-start | bytes 589832 | tf_op jit(solution)/shard_map/ppermute | solution.py:148
  246.2 31.7 %collective-permute-start.46 = (bf16[3,256,128]{2,1,0:T(8,128)(2,1)}, bf16[3,256,128]{2,1,0:T(8,128)(2,1)S(1)}, u32[]{:S(2)}, u32[]{:S(2)}) collective-permute-start(bf16[3,256,128]{2,1,0:T(8,128)(2,1)} %get-tuple-element.112), channel_id=1, source_target_pairs={{0,3},{1,2},{2,1},{3,0},{4,7},{5,6},{6,5},{7,4},{8,11},{9,10},{10,... | collective-permute-start | bytes 589832 | tf_op jit(solution)/shard_map/ppermute | solution.py:148
  253.8 27.3 %collective-permute-start.47 = (bf16[3,256,128]{2,1,0:T(8,128)(2,1)}, bf16[3,256,128]{2,1,0:T(8,128)(2,1)S(1)}, u32[]{:S(2)}, u32[]{:S(2)}) collective-permute-start(bf16[3,256,128]{2,1,0:T(8,128)(2,1)} %get-tuple-element.113), channel_id=1, source_target_pairs={{0,4},{1,5},{2,6},{3,7},{4,0},{5,1},{6,2},{7,3},{8,12},{9,13},{10,... | collective-permute-start | bytes 589832 | tf_op jit(solution)/shard_map/ppermute | solution.py:148
  266.6 15.3 %collective-permute-start.48 = (bf16[3,256,128]{2,1,0:T(8,128)(2,1)}, bf16[3,256,128]{2,1,0:T(8,128)(2,1)S(1)}, u32[]{:S(2)}, u32[]{:S(2)}) collective-permute-start(bf16[3,256,128]{2,1,0:T(8,128)(2,1)} %get-tuple-element.114), channel_id=1, source_target_pairs={{0,5},{1,4},{2,7},{3,6},{4,1},{5,0},{6,3},{7,2},{8,13},{9,12},{10,... | collective-permute-start | bytes 589832 | tf_op jit(solution)/shard_map/ppermute | solution.py:148
  266.6 19.4 %collective-permute-start.49 = (bf16[3,256,128]{2,1,0:T(8,128)(2,1)}, bf16[3,256,128]{2,1,0:T(8,128)(2,1)S(1)}, u32[]{:S(2)}, u32[]{:S(2)}) collective-permute-start(bf16[3,256,128]{2,1,0:T(8,128)(2,1)} %get-tuple-element.115), channel_id=1, source_target_pairs={{0,6},{1,7},{2,4},{3,5},{4,2},{5,3},{6,0},{7,1},{8,14},{9,15},{10,... | collective-permute-start | bytes 589832 | tf_op jit(solution)/shard_map/ppermute | solution.py:148
  276.5 43.6 %collective-permute-start.58 = (bf16[6,256,128]{2,1,0:T(8,128)(2,1)}, bf16[6,256,128]{2,1,0:T(8,128)(2,1)S(1)}, u32[]{:S(2)}, u32[]{:S(2)}) collective-permute-start(bf16[6,256,128]{2,1,0:T(8,128)(2,1)} %get-tuple-element.126), channel_id=1, source_target_pairs={{0,1},{1,0},{2,3},{3,2},{4,5},{5,4},{6,7},{7,6},{8,9},{9,8},{10,11... | collective-permute-start | bytes 1179656 | tf_op jit(solution)/shard_map/ppermute | solution.py:148
  278.6 45.2 %collective-permute-start.59 = (bf16[6,256,128]{2,1,0:T(8,128)(2,1)}, bf16[6,256,128]{2,1,0:T(8,128)(2,1)S(1)}, u32[]{:S(2)}, u32[]{:S(2)}) collective-permute-start(bf16[6,256,128]{2,1,0:T(8,128)(2,1)} %get-tuple-element.127), channel_id=1, source_target_pairs={{0,2},{1,3},{2,0},{3,1},{4,6},{5,7},{6,4},{7,5},{8,10},{9,11},{10,... | collective-permute-start | bytes 1179656 | tf_op jit(solution)/shard_map/ppermute | solution.py:148
  281.8 42.0 %collective-permute-start.60 = (bf16[6,256,128]{2,1,0:T(8,128)(2,1)}, bf16[6,256,128]{2,1,0:T(8,128)(2,1)S(1)}, u32[]{:S(2)}, u32[]{:S(2)}) collective-permute-start(bf16[6,256,128]{2,1,0:T(8,128)(2,1)} %get-tuple-element.128), channel_id=1, source_target_pairs={{0,3},{1,2},{2,1},{3,0},{4,7},{5,6},{6,5},{7,4},{8,11},{9,10},{10,... | collective-permute-start | bytes 1179656 | tf_op jit(solution)/shard_map/ppermute | solution.py:148
  281.9 43.4 %collective-permute-start.61 = (bf16[6,256,128]{2,1,0:T(8,128)(2,1)}, bf16[6,256,128]{2,1,0:T(8,128)(2,1)S(1)}, u32[]{:S(2)}, u32[]{:S(2)}) collective-permute-start(bf16[6,256,128]{2,1,0:T(8,128)(2,1)} %get-tuple-element.129), channel_id=1, source_target_pairs={{0,4},{1,5},{2,6},{3,7},{4,0},{5,1},{6,2},{7,3},{8,12},{9,13},{10,... | collective-permute-start | bytes 1179656 | tf_op jit(solution)/shard_map/ppermute | solution.py:148
  286.0 34.0 %collective-permute-start.50 = (bf16[3,256,128]{2,1,0:T(8,128)(2,1)S(1)}, bf16[3,256,128]{2,1,0:T(8,128)(2,1)S(1)}, u32[]{:S(2)}, u32[]{:S(2)}) collective-permute-start(bf16[3,256,128]{2,1,0:T(8,128)(2,1)S(1)} %copy-done.57), channel_id=1, source_target_pairs={{0,7},{1,6},{2,5},{3,4},{4,3},{5,2},{6,1},{7,0},{8,15},{9,14},{10,... | collective-permute-start | bytes 589832 | tf_op jit(solution)/shard_map/ppermute | solution.py:148
  320.1 22.3 %collective-permute-start.62 = (bf16[6,256,128]{2,1,0:T(8,128)(2,1)}, bf16[6,256,128]{2,1,0:T(8,128)(2,1)S(1)}, u32[]{:S(2)}, u32[]{:S(2)}) collective-permute-start(bf16[6,256,128]{2,1,0:T(8,128)(2,1)} %get-tuple-element.130), channel_id=1, source_target_pairs={{0,5},{1,4},{2,7},{3,6},{4,1},{5,0},{6,3},{7,2},{8,13},{9,12},{10,... | collective-permute-start | bytes 1179656 | tf_op jit(solution)/shard_map/ppermute | solution.py:148
  320.1 39.1 %collective-permute-start.63 = (bf16[6,256,128]{2,1,0:T(8,128)(2,1)}, bf16[6,256,128]{2,1,0:T(8,128)(2,1)S(1)}, u32[]{:S(2)}, u32[]{:S(2)}) collective-permute-start(bf16[6,256,128]{2,1,0:T(8,128)(2,1)} %get-tuple-element.131), channel_id=1, source_target_pairs={{0,6},{1,7},{2,4},{3,5},{4,2},{5,3},{6,0},{7,1},{8,14},{9,15},{10,... | collective-permute-start | bytes 1179656 | tf_op jit(solution)/shard_map/ppermute | solution.py:148
  323.8 59.8 %collective-permute-start.64 = (bf16[6,256,128]{2,1,0:T(8,128)(2,1)}, bf16[6,256,128]{2,1,0:T(8,128)(2,1)S(1)}, u32[]{:S(2)}, u32[]{:S(2)}) collective-permute-start(bf16[6,256,128]{2,1,0:T(8,128)(2,1)} %get-tuple-element.132), channel_id=1, source_target_pairs={{0,7},{1,6},{2,5},{3,4},{4,3},{5,2},{6,1},{7,0},{8,15},{9,14},{10,... | collective-permute-start | bytes 1179656 | tf_op jit(solution)/shard_map/ppermute | solution.py:148
  323.8 59.8 %collective-permute-start.51 = (bf16[6,256,128]{2,1,0:T(8,128)(2,1)}, bf16[6,256,128]{2,1,0:T(8,128)(2,1)S(1)}, u32[]{:S(2)}, u32[]{:S(2)}) collective-permute-start(bf16[6,256,128]{2,1,0:T(8,128)(2,1)} %get-tuple-element.118), channel_id=1, source_target_pairs={{0,1},{1,0},{2,3},{3,2},{4,5},{5,4},{6,7},{7,6},{8,9},{9,8},{10,11... | collective-permute-start | bytes 1179656 | tf_op jit(solution)/shard_map/ppermute | solution.py:148
  325.4 58.8 %collective-permute-start.52 = (bf16[6,256,128]{2,1,0:T(8,128)(2,1)}, bf16[6,256,128]{2,1,0:T(8,128)(2,1)}, u32[]{:S(2)}, u32[]{:S(2)}) collective-permute-start(bf16[6,256,128]{2,1,0:T(8,128)(2,1)} %get-tuple-element.119), channel_id=1, source_target_pairs={{0,2},{1,3},{2,0},{3,1},{4,6},{5,7},{6,4},{7,5},{8,10},{9,11},{10,... | collective-permute-start | bytes 1179656 | tf_op jit(solution)/shard_map/ppermute | solution.py:148
  342.4 48.4 %collective-permute-start.53 = (bf16[6,256,128]{2,1,0:T(8,128)(2,1)}, bf16[6,256,128]{2,1,0:T(8,128)(2,1)}, u32[]{:S(2)}, u32[]{:S(2)}) collective-permute-start(bf16[6,256,128]{2,1,0:T(8,128)(2,1)} %get-tuple-element.120), channel_id=1, source_target_pairs={{0,3},{1,2},{2,1},{3,0},{4,7},{5,6},{6,5},{7,4},{8,11},{9,10},{10,... | collective-permute-start | bytes 1179656 | tf_op jit(solution)/shard_map/ppermute | solution.py:148
  359.2 43.1 %collective-permute-start.54 = (bf16[6,256,128]{2,1,0:T(8,128)(2,1)}, bf16[6,256,128]{2,1,0:T(8,128)(2,1)}, u32[]{:S(2)}, u32[]{:S(2)}) collective-permute-start(bf16[6,256,128]{2,1,0:T(8,128)(2,1)} %get-tuple-element.121), channel_id=1, source_target_pairs={{0,4},{1,5},{2,6},{3,7},{4,0},{5,1},{6,2},{7,3},{8,12},{9,13},{10,... | collective-permute-start | bytes 1179656 | tf_op jit(solution)/shard_map/ppermute | solution.py:148
  383.6 29.9 %collective-permute-start.55 = (bf16[6,256,128]{2,1,0:T(8,128)(2,1)}, bf16[6,256,128]{2,1,0:T(8,128)(2,1)}, u32[]{:S(2)}, u32[]{:S(2)}) collective-permute-start(bf16[6,256,128]{2,1,0:T(8,128)(2,1)} %get-tuple-element.122), channel_id=1, source_target_pairs={{0,5},{1,4},{2,7},{3,6},{4,1},{5,0},{6,3},{7,2},{8,13},{9,12},{10,... | collective-permute-start | bytes 1179656 | tf_op jit(solution)/shard_map/ppermute | solution.py:148
  383.6 44.1 %collective-permute-start.56 = (bf16[6,256,128]{2,1,0:T(8,128)(2,1)}, bf16[6,256,128]{2,1,0:T(8,128)(2,1)}, u32[]{:S(2)}, u32[]{:S(2)}) collective-permute-start(bf16[6,256,128]{2,1,0:T(8,128)(2,1)} %get-tuple-element.123), channel_id=1, source_target_pairs={{0,6},{1,7},{2,4},{3,5},{4,2},{5,3},{6,0},{7,1},{8,14},{9,15},{10,... | collective-permute-start | bytes 1179656 | tf_op jit(solution)/shard_map/ppermute | solution.py:148
  384.2 49.1 %collective-permute-start.57 = (bf16[6,256,128]{2,1,0:T(8,128)(2,1)}, bf16[6,256,128]{2,1,0:T(8,128)(2,1)}, u32[]{:S(2)}, u32[]{:S(2)}) collective-permute-start(bf16[6,256,128]{2,1,0:T(8,128)(2,1)} %get-tuple-element.124), channel_id=1, source_target_pairs={{0,7},{1,6},{2,5},{3,4},{4,3},{5,2},{6,1},{7,0},{8,15},{9,14},{10,... | collective-permute-start | bytes 1179656 | tf_op jit(solution)/shard_map/ppermute | solution.py:148
  390.8 68.8 %collective-permute-start.39 = (bf16[1,256,128]{2,1,0:T(8,128)(2,1)}, bf16[1,256,128]{2,1,0:T(8,128)(2,1)S(1)}, u32[]{:S(2)}, u32[]{:S(2)}) collective-permute-start(bf16[1,256,128]{2,1,0:T(8,128)(2,1)} %get-tuple-element.104), channel_id=1, source_target_pairs={{0,3},{1,2},{2,1},{3,0},{4,7},{5,6},{6,5},{7,4},{8,11},{9,10},{10,... | collective-permute-start | bytes 196616 | tf_op jit(solution)/shard_map/ppermute | solution.py:148
  402.3 57.3 %collective-permute-start.40 = (bf16[1,256,128]{2,1,0:T(8,128)(2,1)}, bf16[1,256,128]{2,1,0:T(8,128)(2,1)}, u32[]{:S(2)}, u32[]{:S(2)}) collective-permute-start(bf16[1,256,128]{2,1,0:T(8,128)(2,1)} %get-tuple-element.105), channel_id=1, source_target_pairs={{0,4},{1,5},{2,6},{3,7},{4,0},{5,1},{6,2},{7,3},{8,12},{9,13},{10,... | collective-permute-start | bytes 196616 | tf_op jit(solution)/shard_map/ppermute | solution.py:148
  413.5 46.1 %collective-permute-start.41 = (bf16[1,256,128]{2,1,0:T(8,128)(2,1)}, bf16[1,256,128]{2,1,0:T(8,128)(2,1)}, u32[]{:S(2)}, u32[]{:S(2)}) collective-permute-start(bf16[1,256,128]{2,1,0:T(8,128)(2,1)} %get-tuple-element.106), channel_id=1, source_target_pairs={{0,5},{1,4},{2,7},{3,6},{4,1},{5,0},{6,3},{7,2},{8,13},{9,12},{10,... | collective-permute-start | bytes 196616 | tf_op jit(solution)/shard_map/ppermute | solution.py:148
  427.7 31.9 %collective-permute-start.42 = (bf16[1,256,128]{2,1,0:T(8,128)(2,1)}, bf16[1,256,128]{2,1,0:T(8,128)(2,1)}, u32[]{:S(2)}, u32[]{:S(2)}) collective-permute-start(bf16[1,256,128]{2,1,0:T(8,128)(2,1)} %get-tuple-element.107), channel_id=1, source_target_pairs={{0,6},{1,7},{2,4},{3,5},{4,2},{5,3},{6,0},{7,1},{8,14},{9,15},{10,... | collective-permute-start | bytes 196616 | tf_op jit(solution)/shard_map/ppermute | solution.py:148
  433.3 26.3 %collective-permute-start.43 = (bf16[1,256,128]{2,1,0:T(8,128)(2,1)}, bf16[1,256,128]{2,1,0:T(8,128)(2,1)}, u32[]{:S(2)}, u32[]{:S(2)}) collective-permute-start(bf16[1,256,128]{2,1,0:T(8,128)(2,1)} %get-tuple-element.108), channel_id=1, source_target_pairs={{0,7},{1,6},{2,5},{3,4},{4,3},{5,2},{6,1},{7,0},{8,15},{9,14},{10,... | collective-permute-start | bytes 196616 | tf_op jit(solution)/shard_map/ppermute | solution.py:148
  (64 other events, 1902.9 us)
